TPU v7x, 512 devices: a whole 4x4x16 slice. The times are simulated.
512 devices in a mesh: gx: 8 (over z_lo), gy: 16 (over x, z_hi, core), band: 4 (over y).
Axes of the slice: x: 4, y: 4, z: 16 (z_hi: 2, z_lo: 8; z = z_hi * 8 + z_lo), core: 2. Of those that a mesh axis runs over, the one named last changes fastest.
Arguments:
- orbitals: float32 [2, 16, 64, 192, 128], P(None, 'band', 'gx', 'gy'), may hold values from -3 to 3
- external: float32 [64, 192, 128], P('gx', 'gy'), may hold values from 2 to 6
Outputs:
- orbitals_next: float32 [2, 16, 64, 192, 128], P(None, 'band', 'gx', 'gy')
- potential_next: float32 [64, 192, 128], P('gx', 'gy')
All inputs are finite; a program needn't handle non-finite values.
Results may differ from a plain program's by a relative error of at most 0.00002.
Values sent between devices are 32-bit elements; how exact they have to be, the bound alone decides.
A program may use at most 64 MiB of HBM per device.

v0:
```python
import jax
import jax.numpy as jnp
from jax import lax
from jax.sharding import PartitionSpec as P

step_length = 0.15
exchange_coef = 0.7386
centre_weight = -2.5
near_weight = 4.0 / 3.0
far_weight = -1.0 / 12.0


def copy_for_each(array, axis):
    length = lax.axis_size(axis)
    return lax.all_to_all(
        jnp.broadcast_to(array[None], (length, *array.shape)), axis, 0, 0, tiled=True
    )


def taken_together(array, axis):
    everything = copy_for_each(array, axis)
    return jnp.sum(everything, axis=0)


def padded_2(array, sides, width):
    edges = {}
    for axis, dim in sides:
        size, length = (lax.axis_size(axis), array.shape[dim])
        up = [(i, (i + 1) % size) for i in range(size - 1)]
        last = lax.slice_in_dim(array, length - width, length, axis=dim)
        first = lax.slice_in_dim(array, 0, width, axis=dim)
        edges[dim] = (
            lax.ppermute(last, axis, up),
            lax.ppermute(first, axis, [(b, a) for a, b in up]),
        )
    done = []
    for _, dim in sides:
        low, high = edges[dim]
        around = [(width, width) if d in done else (0, 0) for d in range(array.ndim)]
        array = jnp.concatenate([jnp.pad(low, around), array, jnp.pad(high, around)], axis=dim)
        done.append(dim)
    return array


def shifted(padded, which_axis, offset):
    dimensions = padded.ndim
    selector = []
    for position in range(dimensions):
        if position < dimensions - 3:
            selector.append(slice(None))
        elif position == which_axis:
            selector.append(slice(2 + offset, padded.shape[position] - 2 + offset))
        else:
            selector.append(slice(2, padded.shape[position] - 2))
    return padded[tuple(selector)]


def laplacian(padded):
    dimensions = padded.ndim
    centre = shifted(padded, dimensions - 1, 0)
    summed = 3.0 * centre_weight * centre
    for which_axis in range(dimensions - 3, dimensions):
        summed = summed + near_weight * (
            shifted(padded, which_axis, 1) + shifted(padded, which_axis, -1)
        )
        summed = summed + far_weight * (
            shifted(padded, which_axis, 2) + shifted(padded, which_axis, -2)
        )
    return summed


def taylor(values, apply_fn, interval):
    summed = values
    taylor_term = values
    for degree in range(1, 5):
        image = apply_fn(taylor_term)
        factor = interval / degree
        taylor_term = jnp.stack([factor * image[1], -factor * image[0]])
        summed = summed + taylor_term
    return summed


def taylor_pair(values, apply_fn, first_len, second_len):
    first_sum = values
    second_sum = values
    taylor_term = values
    for degree in range(1, 5):
        image = apply_fn(taylor_term)
        factor = 1.0 / degree
        taylor_term = jnp.stack([factor * image[1], -factor * image[0]])
        first_sum = first_sum + first_len**degree * taylor_term
        second_sum = second_sum + second_len**degree * taylor_term
    return (first_sum, second_sum)


def density_potential(values, external):
    local_density = jnp.sum(values * values, axis=(0, 1))
    summed = taken_together(local_density, "band")
    return external - exchange_coef * jnp.cbrt(summed)


def apply_each(values, potential):
    padded = padded_2(values, (("gx", 2), ("gy", 3)), 2)
    padded = jnp.pad(padded, ((0, 0), (0, 0), (0, 0), (0, 0), (2, 2)))
    return -0.5 * laplacian(padded) + potential * values


def body(orbitals, external):
    potential_now = density_potential(orbitals, external)

    def apply_now(values):
        return apply_each(values, potential_now)

    predicted, halfway = taylor_pair(orbitals, apply_now, step_length, step_length / 2)
    potential_next = density_potential(predicted, external)

    def apply_next(values):
        return apply_each(values, potential_next)

    result = taylor(halfway, apply_next, step_length / 2)
    return (result, potential_next)


def solution(mesh):
    in_specs = (P(None, "band", "gx", "gy", None), P("gx", "gy", None))
    out_specs = (P(None, "band", "gx", "gy", None), P("gx", "gy", None))
    return jax.shard_map(body, mesh=mesh, in_specs=in_specs, out_specs=out_specs, check_vma=False)
```

profile of v0, /device:TPU:103, one launch (start us, length us, event | category | flops | bytes accessed | tf_op | source)
XLA Modules:
  0.0 237.6 jit_solution(16467957263037047813)
XLA Ops:
  1.6 13.3 %collective-permute-start.3 = (f32[2,4,8,2,128]{4,2,3,1,0:T(8,128)S(1)}, f32[2,4,8,2,128]{4,2,3,1,0:T(8,128)S(1)}, u32[]{:S(2)}, u32[]{:S(2)}) collective-permute-start(f32[2,4,8,2,128]{4,2,3,1,0:T(8,128)S(1)} %get-tuple-element.64), channel_id=1, source_target_pairs={{0,4},{4,8},{8,12},{12,16},{16,20},{20,24},{24,28},{28,32},{32,36}... | collective-permute-start | bytes 196616 | tf_op jit(solution)/shard_map/ppermute | solution.py:33
  18.0 2.6 %collective-permute-start = (f32[2,4,2,12,128]{4,2,3,1,0:T(2,128)S(1)}, f32[2,4,2,12,128]{4,2,3,1,0:T(2,128)}, u32[]{:S(2)}, u32[]{:S(2)}) collective-permute-start(f32[2,4,2,12,128]{4,2,3,1,0:T(2,128)S(1)} %get-tuple-element.62), channel_id=1, source_target_pairs={{64,0},{128,64},{192,128},{256,192},{320,256},{384,320},{448,384},... | collective-permute-start | bytes 294920 | tf_op jit(solution)/shard_map/ppermute | solution.py:34
  20.7 3.9 %collective-permute-start.1 = (f32[2,4,2,12,128]{4,2,3,1,0:T(2,128)S(1)}, f32[2,4,2,12,128]{4,2,3,1,0:T(2,128)}, u32[]{:S(2)}, u32[]{:S(2)}) collective-permute-start(f32[2,4,2,12,128]{4,2,3,1,0:T(2,128)S(1)} %get-tuple-element.63), channel_id=1, source_target_pairs={{0,64},{64,128},{128,192},{192,256},{256,320},{320,384},{384,448},... | collective-permute-start | bytes 294920 | tf_op jit(solution)/shard_map/ppermute | solution.py:33
  26.3 4.2 %all-to-all-start = ((f32[4,8,12,128]{3,1,2,0:T(8,128)}), f32[4,8,12,128]{3,1,2,0:T(8,128)}, u32[]{:S(2)}, u32[]{:S(2)}) async-start(f32[4,8,12,128]{3,1,2,0:T(8,128)} %broadcast_in_dim.4), calls=%async_computation | async-start | bytes 393216 | tf_op jit(solution)/shard_map/all_to_all | solution.py:15
  33.4 2.3 all-to-all-done
  42.2 3.4 %collective-permute-start.4 = (f32[2,4,2,12,128]{4,2,3,1,0:T(2,128)S(1)}, f32[2,4,2,12,128]{4,2,3,1,0:T(2,128)S(1)}, u32[]{:S(2)}, u32[]{:S(2)}) collective-permute-start(f32[2,4,2,12,128]{4,2,3,1,0:T(2,128)S(1)} %get-tuple-element.55), channel_id=1, source_target_pairs={{64,0},{128,64},{192,128},{256,192},{320,256},{384,320},{448,384},... | collective-permute-start | bytes 294920 | tf_op jit(solution)/shard_map/ppermute | solution.py:34
  45.6 14.9 %collective-permute-start.7 = (f32[2,4,8,2,128]{4,2,3,1,0:T(8,128)S(1)}, f32[2,4,8,2,128]{4,2,3,1,0:T(8,128)S(1)}, u32[]{:S(2)}, u32[]{:S(2)}) collective-permute-start(f32[2,4,8,2,128]{4,2,3,1,0:T(8,128)S(1)} %get-tuple-element.56), channel_id=1, source_target_pairs={{0,4},{4,8},{8,12},{12,16},{16,20},{20,24},{24,28},{28,32},{32,36}... | collective-permute-start | bytes 196616 | tf_op jit(solution)/shard_map/ppermute | solution.py:33
  62.8 12.7 %collective-permute-done.6 = f32[2,4,8,2,128]{4,2,3,1,0:T(8,128)S(1)} collective-permute-done((f32[2,4,8,2,128]{4,2,3,1,0:T(8,128)S(1)}, f32[2,4,8,2,128]{4,2,3,1,0:T(8,128)S(1)}, u32[]{:S(2)}, u32[]{:S(2)}) %collective-permute-start.6) | collective-permute-done | bytes 65568 | tf_op jit(solution)/shard_map/ppermute | solution.py:34
  77.5 3.7 %collective-permute-start.9 = (f32[2,4,2,12,128]{4,2,3,1,0:T(2,128)S(1)}, f32[2,4,2,12,128]{4,2,3,1,0:T(2,128)S(1)}, u32[]{:S(2)}, u32[]{:S(2)}) collective-permute-start(f32[2,4,2,12,128]{4,2,3,1,0:T(2,128)S(1)} %get-tuple-element.46), channel_id=1, source_target_pairs={{0,64},{64,128},{128,192},{192,256},{256,320},{320,384},{384,448},... | collective-permute-start | bytes 294920 | tf_op jit(solution)/shard_map/ppermute | solution.py:33
  85.2 2.3 collective-permute-start.10
  87.6 13.8 %collective-permute-done.10 = f32[2,4,8,2,128]{4,2,3,1,0:T(8,128)S(1)} collective-permute-done((f32[2,4,8,2,128]{4,2,3,1,0:T(8,128)S(1)}, f32[2,4,8,2,128]{4,2,3,1,0:T(8,128)S(1)}, u32[]{:S(2)}, u32[]{:S(2)}) %collective-permute-start.10) | collective-permute-done | bytes 65568 | tf_op jit(solution)/shard_map/ppermute | solution.py:34
  103.4 2.9 %collective-permute-start.13 = (f32[2,4,2,12,128]{4,2,3,1,0:T(2,128)S(1)}, f32[2,4,2,12,128]{4,2,3,1,0:T(2,128)S(1)}, u32[]{:S(2)}, u32[]{:S(2)}) collective-permute-start(f32[2,4,2,12,128]{4,2,3,1,0:T(2,128)S(1)} %get-tuple-element.38), channel_id=1, source_target_pairs={{0,64},{64,128},{128,192},{192,256},{256,320},{320,384},{384,448},... | collective-permute-start | bytes 294920 | tf_op jit(solution)/shard_map/ppermute | solution.py:33
  106.3 2.3 collective-permute-start.12
  108.7 2.3 collective-permute-start.15
  113.1 12.4 %collective-permute-done.14 = f32[2,4,8,2,128]{4,2,3,1,0:T(8,128)S(1)} collective-permute-done((f32[2,4,8,2,128]{4,2,3,1,0:T(8,128)S(1)}, f32[2,4,8,2,128]{4,2,3,1,0:T(8,128)S(1)}, u32[]{:S(2)}, u32[]{:S(2)}) %collective-permute-start.14) | collective-permute-done | bytes 65568 | tf_op jit(solution)/shard_map/ppermute | solution.py:34
  129.7 4.6 %collective-permute-start.17 = (f32[2,4,2,12,128]{4,2,3,1,0:T(2,128)S(1)}, f32[2,4,2,12,128]{4,2,3,1,0:T(2,128)S(1)}, u32[]{:S(2)}, u32[]{:S(2)}) collective-permute-start(f32[2,4,2,12,128]{4,2,3,1,0:T(2,128)S(1)} %get-tuple-element.33), channel_id=1, source_target_pairs={{0,64},{64,128},{128,192},{192,256},{256,320},{320,384},{384,448},... | collective-permute-start | bytes 294920 | tf_op jit(solution)/shard_map/ppermute | solution.py:33
  134.3 2.4 %collective-permute-start.19 = (f32[2,4,8,2,128]{4,2,3,1,0:T(8,128)S(1)}, f32[2,4,8,2,128]{4,2,3,1,0:T(8,128)S(1)}, u32[]{:S(2)}, u32[]{:S(2)}) collective-permute-start(f32[2,4,8,2,128]{4,2,3,1,0:T(8,128)S(1)} %get-tuple-element.30), channel_id=1, source_target_pairs={{0,4},{4,8},{8,12},{12,16},{16,20},{20,24},{24,28},{28,32},{32,36}... | collective-permute-start | bytes 196616 | tf_op jit(solution)/shard_map/ppermute | solution.py:33
  139.4 3.5 %all-to-all-start.1 = ((f32[4,8,12,128]{3,1,2,0:T(8,128)}), f32[4,8,12,128]{3,1,2,0:T(8,128)S(1)}, u32[]{:S(2)}, u32[]{:S(2)}) async-start(f32[4,8,12,128]{3,1,2,0:T(8,128)} %broadcast_in_dim.5), calls=%async_computation.1 | async-start | bytes 393216 | tf_op jit(solution)/shard_map/all_to_all | solution.py:15
  142.9 8.8 %collective-permute-done.18 = f32[2,4,8,2,128]{4,2,3,1,0:T(8,128)S(1)} collective-permute-done((f32[2,4,8,2,128]{4,2,3,1,0:T(8,128)S(1)}, f32[2,4,8,2,128]{4,2,3,1,0:T(8,128)S(1)}, u32[]{:S(2)}, u32[]{:S(2)}) %collective-permute-start.18) | collective-permute-done | bytes 65568 | tf_op jit(solution)/shard_map/ppermute | solution.py:34
  153.9 2.7 %collective-permute-start.21 = (f32[2,4,2,12,128]{4,2,3,1,0:T(2,128)S(1)}, f32[2,4,2,12,128]{4,2,3,1,0:T(2,128)S(1)}, u32[]{:S(2)}, u32[]{:S(2)}) collective-permute-start(f32[2,4,2,12,128]{4,2,3,1,0:T(2,128)S(1)} %get-tuple-element.24), channel_id=1, source_target_pairs={{0,64},{64,128},{128,192},{192,256},{256,320},{320,384},{384,448},... | collective-permute-start | bytes 294920 | tf_op jit(solution)/shard_map/ppermute | solution.py:33
  156.6 2.6 %collective-permute-start.20 = (f32[2,4,2,12,128]{4,2,3,1,0:T(2,128)S(1)}, f32[2,4,2,12,128]{4,2,3,1,0:T(2,128)S(1)}, u32[]{:S(2)}, u32[]{:S(2)}) collective-permute-start(f32[2,4,2,12,128]{4,2,3,1,0:T(2,128)S(1)} %get-tuple-element.25), channel_id=1, source_target_pairs={{64,0},{128,64},{192,128},{256,192},{320,256},{384,320},{448,384},... | collective-permute-start | bytes 294920 | tf_op jit(solution)/shard_map/ppermute | solution.py:34
  159.2 9.1 %collective-permute-start.23 = (f32[2,4,8,2,128]{4,2,3,1,0:T(8,128)S(1)}, f32[2,4,8,2,128]{4,2,3,1,0:T(8,128)S(1)}, u32[]{:S(2)}, u32[]{:S(2)}) collective-permute-start(f32[2,4,8,2,128]{4,2,3,1,0:T(8,128)S(1)} %get-tuple-element.26), channel_id=1, source_target_pairs={{0,4},{4,8},{8,12},{12,16},{16,20},{20,24},{24,28},{28,32},{32,36}... | collective-permute-start | bytes 196616 | tf_op jit(solution)/shard_map/ppermute | solution.py:33
  170.3 14.0 %collective-permute-done.22 = f32[2,4,8,2,128]{4,2,3,1,0:T(8,128)S(1)} collective-permute-done((f32[2,4,8,2,128]{4,2,3,1,0:T(8,128)S(1)}, f32[2,4,8,2,128]{4,2,3,1,0:T(8,128)S(1)}, u32[]{:S(2)}, u32[]{:S(2)}) %collective-permute-start.22) | collective-permute-done | bytes 65568 | tf_op jit(solution)/shard_map/ppermute | solution.py:34
  186.3 2.9 %collective-permute-start.25 = (f32[2,4,2,12,128]{4,2,3,1,0:T(2,128)S(1)}, f32[2,4,2,12,128]{4,2,3,1,0:T(2,128)S(1)}, u32[]{:S(2)}, u32[]{:S(2)}) collective-permute-start(f32[2,4,2,12,128]{4,2,3,1,0:T(2,128)S(1)} %get-tuple-element.16), channel_id=1, source_target_pairs={{0,64},{64,128},{128,192},{192,256},{256,320},{320,384},{384,448},... | collective-permute-start | bytes 294920 | tf_op jit(solution)/shard_map/ppermute | solution.py:33
  189.2 2.4 %collective-permute-start.24 = (f32[2,4,2,12,128]{4,2,3,1,0:T(2,128)S(1)}, f32[2,4,2,12,128]{4,2,3,1,0:T(2,128)S(1)}, u32[]{:S(2)}, u32[]{:S(2)}) collective-permute-start(f32[2,4,2,12,128]{4,2,3,1,0:T(2,128)S(1)} %get-tuple-element.17), channel_id=1, source_target_pairs={{64,0},{128,64},{192,128},{256,192},{320,256},{384,320},{448,384},... | collective-permute-start | bytes 294920 | tf_op jit(solution)/shard_map/ppermute | solution.py:34
  191.7 2.2 collective-permute-start.27
  193.9 2.1 collective-permute-start.26
  196.0 13.6 %collective-permute-done.26 = f32[2,4,8,2,128]{4,2,3,1,0:T(8,128)S(1)} collective-permute-done((f32[2,4,8,2,128]{4,2,3,1,0:T(8,128)S(1)}, f32[2,4,8,2,128]{4,2,3,1,0:T(8,128)S(1)}, u32[]{:S(2)}, u32[]{:S(2)}) %collective-permute-start.26) | collective-permute-done | bytes 65568 | tf_op jit(solution)/shard_map/ppermute | solution.py:34
  211.6 3.1 %collective-permute-start.29 = (f32[2,4,2,12,128]{4,2,3,1,0:T(2,128)S(1)}, f32[2,4,2,12,128]{4,2,3,1,0:T(2,128)S(1)}, u32[]{:S(2)}, u32[]{:S(2)}) collective-permute-start(f32[2,4,2,12,128]{4,2,3,1,0:T(2,128)S(1)} %get-tuple-element.8), channel_id=1, source_target_pairs={{0,64},{64,128},{128,192},{192,256},{256,320},{320,384},{384,448},... | collective-permute-start | bytes 294920 | tf_op jit(solution)/shard_map/ppermute | solution.py:33
  214.8 2.1 collective-permute-start.28
  219.1 2.2 collective-permute-start.30
  221.3 13.4 %collective-permute-done.30 = f32[2,4,8,2,128]{4,2,3,1,0:T(8,128)S(1)} collective-permute-done((f32[2,4,8,2,128]{4,2,3,1,0:T(8,128)S(1)}, f32[2,4,8,2,128]{4,2,3,1,0:T(8,128)S(1)}, u32[]{:S(2)}, u32[]{:S(2)}) %collective-permute-start.30) | collective-permute-done | bytes 65568 | tf_op jit(solution)/shard_map/ppermute | solution.py:34
  (114 shorter events, 47.0 us)
Async XLA Ops:
  1.6 28.9 %collective-permute-start.3 = (f32[2,4,8,2,128]{4,2,3,1,0:T(8,128)S(1)}, f32[2,4,8,2,128]{4,2,3,1,0:T(8,128)S(1)}, u32[]{:S(2)}, u32[]{:S(2)}) collective-permute-start(f32[2,4,8,2,128]{4,2,3,1,0:T(8,128)S(1)} %get-tuple-element.64), channel_id=1, source_target_pairs={{0,4},{4,8},{8,12},{12,16},{16,20},{20,24},{24,28},{28,32},{32,36}... | collective-permute-start | bytes 196616 | tf_op jit(solution)/shard_map/ppermute | solution.py:33
  14.9 15.6 %collective-permute-start.2 = (f32[2,4,8,2,128]{4,2,3,1,0:T(8,128)S(1)}, f32[2,4,8,2,128]{4,2,3,1,0:T(8,128)S(1)}, u32[]{:S(2)}, u32[]{:S(2)}) collective-permute-start(f32[2,4,8,2,128]{4,2,3,1,0:T(8,128)S(1)} %get-tuple-element.65), channel_id=1, source_target_pairs={{4,0},{8,4},{12,8},{16,12},{20,16},{24,20},{28,24},{32,28},{36,32}... | collective-permute-start | bytes 196616 | tf_op jit(solution)/shard_map/ppermute | solution.py:34
  18.0 12.5 %collective-permute-start = (f32[2,4,2,12,128]{4,2,3,1,0:T(2,128)S(1)}, f32[2,4,2,12,128]{4,2,3,1,0:T(2,128)}, u32[]{:S(2)}, u32[]{:S(2)}) collective-permute-start(f32[2,4,2,12,128]{4,2,3,1,0:T(2,128)S(1)} %get-tuple-element.62), channel_id=1, source_target_pairs={{64,0},{128,64},{192,128},{256,192},{320,256},{384,320},{448,384},... | collective-permute-start | bytes 294920 | tf_op jit(solution)/shard_map/ppermute | solution.py:34
  20.7 9.9 %collective-permute-start.1 = (f32[2,4,2,12,128]{4,2,3,1,0:T(2,128)S(1)}, f32[2,4,2,12,128]{4,2,3,1,0:T(2,128)}, u32[]{:S(2)}, u32[]{:S(2)}) collective-permute-start(f32[2,4,2,12,128]{4,2,3,1,0:T(2,128)S(1)} %get-tuple-element.63), channel_id=1, source_target_pairs={{0,64},{64,128},{128,192},{192,256},{256,320},{320,384},{384,448},... | collective-permute-start | bytes 294920 | tf_op jit(solution)/shard_map/ppermute | solution.py:33
  26.3 9.5 %all-to-all-start = ((f32[4,8,12,128]{3,1,2,0:T(8,128)}), f32[4,8,12,128]{3,1,2,0:T(8,128)}, u32[]{:S(2)}, u32[]{:S(2)}) async-start(f32[4,8,12,128]{3,1,2,0:T(8,128)} %broadcast_in_dim.4), calls=%async_computation | async-start | bytes 393216 | tf_op jit(solution)/shard_map/all_to_all | solution.py:15
  40.3 35.3 %collective-permute-start.5 = (f32[2,4,2,12,128]{4,2,3,1,0:T(2,128)S(1)}, f32[2,4,2,12,128]{4,2,3,1,0:T(2,128)S(1)}, u32[]{:S(2)}, u32[]{:S(2)}) collective-permute-start(f32[2,4,2,12,128]{4,2,3,1,0:T(2,128)S(1)} %get-tuple-element.54), channel_id=1, source_target_pairs={{0,64},{64,128},{128,192},{192,256},{256,320},{320,384},{384,448},... | collective-permute-start | bytes 294920 | tf_op jit(solution)/shard_map/ppermute | solution.py:33
  42.2 33.4 %collective-permute-start.4 = (f32[2,4,2,12,128]{4,2,3,1,0:T(2,128)S(1)}, f32[2,4,2,12,128]{4,2,3,1,0:T(2,128)S(1)}, u32[]{:S(2)}, u32[]{:S(2)}) collective-permute-start(f32[2,4,2,12,128]{4,2,3,1,0:T(2,128)S(1)} %get-tuple-element.55), channel_id=1, source_target_pairs={{64,0},{128,64},{192,128},{256,192},{320,256},{384,320},{448,384},... | collective-permute-start | bytes 294920 | tf_op jit(solution)/shard_map/ppermute | solution.py:34
  45.6 17.2 %collective-permute-start.7 = (f32[2,4,8,2,128]{4,2,3,1,0:T(8,128)S(1)}, f32[2,4,8,2,128]{4,2,3,1,0:T(8,128)S(1)}, u32[]{:S(2)}, u32[]{:S(2)}) collective-permute-start(f32[2,4,8,2,128]{4,2,3,1,0:T(8,128)S(1)} %get-tuple-element.56), channel_id=1, source_target_pairs={{0,4},{4,8},{8,12},{12,16},{16,20},{20,24},{24,28},{28,32},{32,36}... | collective-permute-start | bytes 196616 | tf_op jit(solution)/shard_map/ppermute | solution.py:33
  60.5 15.0 %collective-permute-start.6 = (f32[2,4,8,2,128]{4,2,3,1,0:T(8,128)S(1)}, f32[2,4,8,2,128]{4,2,3,1,0:T(8,128)S(1)}, u32[]{:S(2)}, u32[]{:S(2)}) collective-permute-start(f32[2,4,8,2,128]{4,2,3,1,0:T(8,128)S(1)} %get-tuple-element.57), channel_id=1, source_target_pairs={{4,0},{8,4},{12,8},{16,12},{20,16},{24,20},{28,24},{32,28},{36,32}... | collective-permute-start | bytes 196616 | tf_op jit(solution)/shard_map/ppermute | solution.py:34
  77.5 23.8 %collective-permute-start.9 = (f32[2,4,2,12,128]{4,2,3,1,0:T(2,128)S(1)}, f32[2,4,2,12,128]{4,2,3,1,0:T(2,128)S(1)}, u32[]{:S(2)}, u32[]{:S(2)}) collective-permute-start(f32[2,4,2,12,128]{4,2,3,1,0:T(2,128)S(1)} %get-tuple-element.46), channel_id=1, source_target_pairs={{0,64},{64,128},{128,192},{192,256},{256,320},{320,384},{384,448},... | collective-permute-start | bytes 294920 | tf_op jit(solution)/shard_map/ppermute | solution.py:33
  81.2 20.2 %collective-permute-start.8 = (f32[2,4,2,12,128]{4,2,3,1,0:T(2,128)S(1)}, f32[2,4,2,12,128]{4,2,3,1,0:T(2,128)S(1)}, u32[]{:S(2)}, u32[]{:S(2)}) collective-permute-start(f32[2,4,2,12,128]{4,2,3,1,0:T(2,128)S(1)} %get-tuple-element.47), channel_id=1, source_target_pairs={{64,0},{128,64},{192,128},{256,192},{320,256},{384,320},{448,384},... | collective-permute-start | bytes 294920 | tf_op jit(solution)/shard_map/ppermute | solution.py:34
  85.2 16.2 %collective-permute-start.10 = (f32[2,4,8,2,128]{4,2,3,1,0:T(8,128)S(1)}, f32[2,4,8,2,128]{4,2,3,1,0:T(8,128)S(1)}, u32[]{:S(2)}, u32[]{:S(2)}) collective-permute-start(f32[2,4,8,2,128]{4,2,3,1,0:T(8,128)S(1)} %get-tuple-element.49), channel_id=1, source_target_pairs={{4,0},{8,4},{12,8},{16,12},{20,16},{24,20},{28,24},{32,28},{36,32}... | collective-permute-start | bytes 196616 | tf_op jit(solution)/shard_map/ppermute | solution.py:34
  103.4 22.1 %collective-permute-start.13 = (f32[2,4,2,12,128]{4,2,3,1,0:T(2,128)S(1)}, f32[2,4,2,12,128]{4,2,3,1,0:T(2,128)S(1)}, u32[]{:S(2)}, u32[]{:S(2)}) collective-permute-start(f32[2,4,2,12,128]{4,2,3,1,0:T(2,128)S(1)} %get-tuple-element.38), channel_id=1, source_target_pairs={{0,64},{64,128},{128,192},{192,256},{256,320},{320,384},{384,448},... | collective-permute-start | bytes 294920 | tf_op jit(solution)/shard_map/ppermute | solution.py:33
  106.3 19.2 %collective-permute-start.12 = (f32[2,4,2,12,128]{4,2,3,1,0:T(2,128)S(1)}, f32[2,4,2,12,128]{4,2,3,1,0:T(2,128)S(1)}, u32[]{:S(2)}, u32[]{:S(2)}) collective-permute-start(f32[2,4,2,12,128]{4,2,3,1,0:T(2,128)S(1)} %get-tuple-element.39), channel_id=1, source_target_pairs={{64,0},{128,64},{192,128},{256,192},{320,256},{384,320},{448,384},... | collective-permute-start | bytes 294920 | tf_op jit(solution)/shard_map/ppermute | solution.py:34
  111.1 14.4 %collective-permute-start.14 = (f32[2,4,8,2,128]{4,2,3,1,0:T(8,128)S(1)}, f32[2,4,8,2,128]{4,2,3,1,0:T(8,128)S(1)}, u32[]{:S(2)}, u32[]{:S(2)}) collective-permute-start(f32[2,4,8,2,128]{4,2,3,1,0:T(8,128)S(1)} %get-tuple-element.41), channel_id=1, source_target_pairs={{4,0},{8,4},{12,8},{16,12},{20,16},{24,20},{28,24},{32,28},{36,32}... | collective-permute-start | bytes 196616 | tf_op jit(solution)/shard_map/ppermute | solution.py:34
  127.8 24.0 %collective-permute-start.16 = (f32[2,4,2,12,128]{4,2,3,1,0:T(2,128)S(1)}, f32[2,4,2,12,128]{4,2,3,1,0:T(2,128)S(1)}, u32[]{:S(2)}, u32[]{:S(2)}) collective-permute-start(f32[2,4,2,12,128]{4,2,3,1,0:T(2,128)S(1)} %get-tuple-element.32), channel_id=1, source_target_pairs={{64,0},{128,64},{192,128},{256,192},{320,256},{384,320},{448,384},... | collective-permute-start | bytes 294920 | tf_op jit(solution)/shard_map/ppermute | solution.py:34
  129.7 22.1 %collective-permute-start.17 = (f32[2,4,2,12,128]{4,2,3,1,0:T(2,128)S(1)}, f32[2,4,2,12,128]{4,2,3,1,0:T(2,128)S(1)}, u32[]{:S(2)}, u32[]{:S(2)}) collective-permute-start(f32[2,4,2,12,128]{4,2,3,1,0:T(2,128)S(1)} %get-tuple-element.33), channel_id=1, source_target_pairs={{0,64},{64,128},{128,192},{192,256},{256,320},{320,384},{384,448},... | collective-permute-start | bytes 294920 | tf_op jit(solution)/shard_map/ppermute | solution.py:33
  134.3 8.6 %collective-permute-start.19 = (f32[2,4,8,2,128]{4,2,3,1,0:T(8,128)S(1)}, f32[2,4,8,2,128]{4,2,3,1,0:T(8,128)S(1)}, u32[]{:S(2)}, u32[]{:S(2)}) collective-permute-start(f32[2,4,8,2,128]{4,2,3,1,0:T(8,128)S(1)} %get-tuple-element.30), channel_id=1, source_target_pairs={{0,4},{4,8},{8,12},{12,16},{16,20},{20,24},{24,28},{28,32},{32,36}... | collective-permute-start | bytes 196616 | tf_op jit(solution)/shard_map/ppermute | solution.py:33
  136.7 15.0 %collective-permute-start.18 = (f32[2,4,8,2,128]{4,2,3,1,0:T(8,128)S(1)}, f32[2,4,8,2,128]{4,2,3,1,0:T(8,128)S(1)}, u32[]{:S(2)}, u32[]{:S(2)}) collective-permute-start(f32[2,4,8,2,128]{4,2,3,1,0:T(8,128)S(1)} %get-tuple-element.31), channel_id=1, source_target_pairs={{4,0},{8,4},{12,8},{16,12},{20,16},{24,20},{28,24},{32,28},{36,32}... | collective-permute-start | bytes 196616 | tf_op jit(solution)/shard_map/ppermute | solution.py:34
  139.4 13.5 %all-to-all-start.1 = ((f32[4,8,12,128]{3,1,2,0:T(8,128)}), f32[4,8,12,128]{3,1,2,0:T(8,128)S(1)}, u32[]{:S(2)}, u32[]{:S(2)}) async-start(f32[4,8,12,128]{3,1,2,0:T(8,128)} %broadcast_in_dim.5), calls=%async_computation.1 | async-start | bytes 393216 | tf_op jit(solution)/shard_map/all_to_all | solution.py:15
  153.9 30.4 %collective-permute-start.21 = (f32[2,4,2,12,128]{4,2,3,1,0:T(2,128)S(1)}, f32[2,4,2,12,128]{4,2,3,1,0:T(2,128)S(1)}, u32[]{:S(2)}, u32[]{:S(2)}) collective-permute-start(f32[2,4,2,12,128]{4,2,3,1,0:T(2,128)S(1)} %get-tuple-element.24), channel_id=1, source_target_pairs={{0,64},{64,128},{128,192},{192,256},{256,320},{320,384},{384,448},... | collective-permute-start | bytes 294920 | tf_op jit(solution)/shard_map/ppermute | solution.py:33
  156.6 27.8 %collective-permute-start.20 = (f32[2,4,2,12,128]{4,2,3,1,0:T(2,128)S(1)}, f32[2,4,2,12,128]{4,2,3,1,0:T(2,128)S(1)}, u32[]{:S(2)}, u32[]{:S(2)}) collective-permute-start(f32[2,4,2,12,128]{4,2,3,1,0:T(2,128)S(1)} %get-tuple-element.25), channel_id=1, source_target_pairs={{64,0},{128,64},{192,128},{256,192},{320,256},{384,320},{448,384},... | collective-permute-start | bytes 294920 | tf_op jit(solution)/shard_map/ppermute | solution.py:34
  159.2 11.0 %collective-permute-start.23 = (f32[2,4,8,2,128]{4,2,3,1,0:T(8,128)S(1)}, f32[2,4,8,2,128]{4,2,3,1,0:T(8,128)S(1)}, u32[]{:S(2)}, u32[]{:S(2)}) collective-permute-start(f32[2,4,8,2,128]{4,2,3,1,0:T(8,128)S(1)} %get-tuple-element.26), channel_id=1, source_target_pairs={{0,4},{4,8},{8,12},{12,16},{16,20},{20,24},{24,28},{28,32},{32,36}... | collective-permute-start | bytes 196616 | tf_op jit(solution)/shard_map/ppermute | solution.py:33
  168.3 16.0 %collective-permute-start.22 = (f32[2,4,8,2,128]{4,2,3,1,0:T(8,128)S(1)}, f32[2,4,8,2,128]{4,2,3,1,0:T(8,128)S(1)}, u32[]{:S(2)}, u32[]{:S(2)}) collective-permute-start(f32[2,4,8,2,128]{4,2,3,1,0:T(8,128)S(1)} %get-tuple-element.27), channel_id=1, source_target_pairs={{4,0},{8,4},{12,8},{16,12},{20,16},{24,20},{28,24},{32,28},{36,32}... | collective-permute-start | bytes 196616 | tf_op jit(solution)/shard_map/ppermute | solution.py:34
  186.3 23.3 %collective-permute-start.25 = (f32[2,4,2,12,128]{4,2,3,1,0:T(2,128)S(1)}, f32[2,4,2,12,128]{4,2,3,1,0:T(2,128)S(1)}, u32[]{:S(2)}, u32[]{:S(2)}) collective-permute-start(f32[2,4,2,12,128]{4,2,3,1,0:T(2,128)S(1)} %get-tuple-element.16), channel_id=1, source_target_pairs={{0,64},{64,128},{128,192},{192,256},{256,320},{320,384},{384,448},... | collective-permute-start | bytes 294920 | tf_op jit(solution)/shard_map/ppermute | solution.py:33
  189.2 20.4 %collective-permute-start.24 = (f32[2,4,2,12,128]{4,2,3,1,0:T(2,128)S(1)}, f32[2,4,2,12,128]{4,2,3,1,0:T(2,128)S(1)}, u32[]{:S(2)}, u32[]{:S(2)}) collective-permute-start(f32[2,4,2,12,128]{4,2,3,1,0:T(2,128)S(1)} %get-tuple-element.17), channel_id=1, source_target_pairs={{64,0},{128,64},{192,128},{256,192},{320,256},{384,320},{448,384},... | collective-permute-start | bytes 294920 | tf_op jit(solution)/shard_map/ppermute | solution.py:34
  191.7 4.3 %collective-permute-start.27 = (f32[2,4,8,2,128]{4,2,3,1,0:T(8,128)S(1)}, f32[2,4,8,2,128]{4,2,3,1,0:T(8,128)S(1)}, u32[]{:S(2)}, u32[]{:S(2)}) collective-permute-start(f32[2,4,8,2,128]{4,2,3,1,0:T(8,128)S(1)} %get-tuple-element.18), channel_id=1, source_target_pairs={{0,4},{4,8},{8,12},{12,16},{16,20},{20,24},{24,28},{28,32},{32,36}... | collective-permute-start | bytes 196616 | tf_op jit(solution)/shard_map/ppermute | solution.py:33
  193.9 15.8 %collective-permute-start.26 = (f32[2,4,8,2,128]{4,2,3,1,0:T(8,128)S(1)}, f32[2,4,8,2,128]{4,2,3,1,0:T(8,128)S(1)}, u32[]{:S(2)}, u32[]{:S(2)}) collective-permute-start(f32[2,4,8,2,128]{4,2,3,1,0:T(8,128)S(1)} %get-tuple-element.19), channel_id=1, source_target_pairs={{4,0},{8,4},{12,8},{16,12},{20,16},{24,20},{28,24},{32,28},{36,32}... | collective-permute-start | bytes 196616 | tf_op jit(solution)/shard_map/ppermute | solution.py:34
  211.6 23.1 %collective-permute-start.29 = (f32[2,4,2,12,128]{4,2,3,1,0:T(2,128)S(1)}, f32[2,4,2,12,128]{4,2,3,1,0:T(2,128)S(1)}, u32[]{:S(2)}, u32[]{:S(2)}) collective-permute-start(f32[2,4,2,12,128]{4,2,3,1,0:T(2,128)S(1)} %get-tuple-element.8), channel_id=1, source_target_pairs={{0,64},{64,128},{128,192},{192,256},{256,320},{320,384},{384,448},... | collective-permute-start | bytes 294920 | tf_op jit(solution)/shard_map/ppermute | solution.py:33
  214.8 20.0 %collective-permute-start.28 = (f32[2,4,2,12,128]{4,2,3,1,0:T(2,128)S(1)}, f32[2,4,2,12,128]{4,2,3,1,0:T(2,128)S(1)}, u32[]{:S(2)}, u32[]{:S(2)}) collective-permute-start(f32[2,4,2,12,128]{4,2,3,1,0:T(2,128)S(1)} %get-tuple-element.9), channel_id=1, source_target_pairs={{64,0},{128,64},{192,128},{256,192},{320,256},{384,320},{448,384},... | collective-permute-start | bytes 294920 | tf_op jit(solution)/shard_map/ppermute | solution.py:34
  217.0 4.3 %collective-permute-start.31 = (f32[2,4,8,2,128]{4,2,3,1,0:T(8,128)S(1)}, f32[2,4,8,2,128]{4,2,3,1,0:T(8,128)S(1)}, u32[]{:S(2)}, u32[]{:S(2)}) collective-permute-start(f32[2,4,8,2,128]{4,2,3,1,0:T(8,128)S(1)} %get-tuple-element.10), channel_id=1, source_target_pairs={{0,4},{4,8},{8,12},{12,16},{16,20},{20,24},{24,28},{28,32},{32,36}... | collective-permute-start | bytes 196616 | tf_op jit(solution)/shard_map/ppermute | solution.py:33
  219.1 15.7 %collective-permute-start.30 = (f32[2,4,8,2,128]{4,2,3,1,0:T(8,128)S(1)}, f32[2,4,8,2,128]{4,2,3,1,0:T(8,128)S(1)}, u32[]{:S(2)}, u32[]{:S(2)}) collective-permute-start(f32[2,4,8,2,128]{4,2,3,1,0:T(8,128)S(1)} %get-tuple-element.11), channel_id=1, source_target_pairs={{4,0},{8,4},{12,8},{16,12},{20,16},{24,20},{28,24},{32,28},{36,32}... | collective-permute-start | bytes 196616 | tf_op jit(solution)/shard_map/ppermute | solution.py:34
  (5 other events, 135.9 us)
where the time goes:
time: 239 us; the launch traced here: 238 us
  starting transfers between devices  117 us (49%)
  waiting for transfers between devices  91.5 us (38%)
  other arithmetic  22.4 us (9%)
  local copies, waits for them, and re-layouts  4.72 us (2%)
    ppermute x16, waiting for transfers between devices, padded_2(): lax.ppermute(first, axis, [(b, a) for a, b in up])  88.8 us
    ppermute x16, starting transfers between devices, padded_2(): lax.ppermute(last, axis, up)  74 us
    ppermute x16, starting transfers between devices, padded_2(): lax.ppermute(first, axis, [(b, a) for a, b in up])  35.7 us
    concatenate x14, other arithmetic, padded_2(): jnp.concatenate([jnp.pad(low, around), array, jnp.pad(high, around)], axi...  10.1 us
    all_to_all x2, starting transfers between devices, copy_for_each(): lax.all_to_all(jnp.broadcast_to(array[None], (length, *array.shape)), axi...  7.73 us
    add x8, other arithmetic, apply_each(): return -0.5 * laplacian(padded) + potential * values  6.91 us
  transfers between devices with their start and end apart: 34, of which 9 were waited for; matrix products, arithmetic and copies ran while one was open for 3% of the time, Pallas kernels for 0%

commit v1 on v0

v1 whole, which is shorter than its diff:
```python
import functools

import jax
import jax.numpy as jnp
from jax import lax
from jax.experimental import pallas as pl
from jax.experimental.pallas import tpu as pltpu
from jax.sharding import PartitionSpec as P

step_length = 0.15
exchange_coef = 0.7386
centre = 3.75
near_w = -2.0 / 3.0
far_w = 1.0 / 24.0

MESH = pl.DeviceIdType.MESH
F = 8
NX, NY, NZ = 8, 12, 128
H = 8
EX, EY = NX + 2 * H, NY + 2 * H


def cube_root(x):
    safe = jnp.maximum(x, 1e-37)
    y = jnp.exp(jnp.log(safe) * (1.0 / 3.0))
    y = y - (y - safe / (y * y)) * (1.0 / 3.0)
    return jnp.where(x > 1e-37, y, 0.0)


def kernel(orb, ext, out, pot, S, V, D, ys, yr, xs, xr, rs, rr, bs, br):
    gx, gy, band = lax.axis_index("gx"), lax.axis_index("gy"), lax.axis_index("band")
    n_gx, n_gy, n_band = lax.axis_size("gx"), lax.axis_size("gy"), lax.axis_size("band")
    odd = lax.rem(gy, 2)
    y_right = (odd == 0, odd == 1)
    y_gy = (gy + 1 - 2 * odd, jnp.clip(gy - 1 + 2 * odd, 0, n_gy - 1))
    far_there = (gy > 0) & (gy < n_gy - 1)
    x_gx = (jnp.maximum(gx - 1, 0), jnp.minimum(gx + 1, n_gx - 1))
    x_there = (gx > 0, gx < n_gx - 1)

    def at(x=gx, y=gy, b=band):
        return (x, y, b)

    def when_side(side, more=None):
        if side == 0:
            return pl.when(more) if more is not None else (lambda f: f())
        return pl.when(far_there & more) if more is not None else pl.when(far_there)

    bar = pltpu.get_barrier_semaphore()

    def greet(dev):
        pl.semaphore_signal(bar, inc=1, device_id=dev, device_id_type=MESH)

    count = jnp.int32(n_band)
    pl.when(far_there)(lambda: greet(at(y=y_gy[1])))
    count = count + far_there.astype(jnp.int32)
    for d in range(2):
        pl.when(x_there[d])(lambda d=d: greet(at(x=x_gx[d])))
        count = count + x_there[d].astype(jnp.int32)
    for i in range(1, n_band):
        greet(at(b=lax.rem(band + i, n_band)))
    greet(at(y=y_gy[0]))

    def density_of(u):
        return jnp.sum(u * u, axis=0, keepdims=True)

    def own_cells(body, unroll):
        def step(i, carry):
            for j in range(unroll):
                body(lax.div(i, NY // unroll), lax.rem(i, NY // unroll) * unroll + j)
            return carry

        lax.fori_loop(0, NX * (NY // unroll), step, 0)

    def take_in(x, y):
        u = orb[pl.ds(x * NY + y, F, stride=NX * NY), :]
        S[0, H + x, H + y] = u
        D[0, band, x, y] = density_of(u)

    own_cells(take_in, 4)

    zero = jnp.zeros((F, NZ), jnp.float32)

    def clear_x(x0):
        def step(i, carry):
            for slot in range(5):
                for dx in range(2):
                    S[slot, x0 + dx, i] = zero
            return carry

        lax.fori_loop(0, EY, step, 0)

    def clear_y(y0):
        def step(i, carry):
            for slot in range(5):
                for dy in range(2):
                    S[slot, i, y0 + dy] = zero
            return carry

        lax.fori_loop(0, EX, step, 0)

    pl.when(gx == 0)(lambda: clear_x(H - 2))
    pl.when(gx == n_gx - 1)(lambda: clear_x(H + NX))
    pl.when(gy == 0)(lambda: clear_y(H - 2))
    pl.when(gy == n_gy - 1)(lambda: clear_y(H + NY))

    pl.semaphore_wait(bar, count)

    def remote(src, dst, s, r, dev):
        return pltpu.make_async_remote_copy(
            src_ref=src, dst_ref=dst, send_sem=s, recv_sem=r, device_id=dev, device_id_type=MESH
        )

    def ref_of(e):
        return S.at[e] if e < 2 else V.at[e - 2]

    def y_copy(e, side, j):
        buf = ref_of(e)
        src_y = jnp.where(y_right[side], H + NY - 2 * j, H + 2 * (j - 1))
        dst_y = jnp.where(y_right[side], H - 2 * j, H + NY + 2 * (j - 1))
        return remote(
            buf.at[pl.ds(H, NX), pl.ds(src_y, 2)],
            buf.at[pl.ds(H, NX), pl.ds(dst_y, 2)],
            ys.at[e, side, j - 1],
            yr.at[e, side, j - 1],
            at(y=y_gy[side]),
        )

    def x_copy(e, d):
        buf = ref_of(e)
        depth = 8 if e < 2 else 6
        src_x = H if d == 0 else H + NX - depth
        dst_x = H + NX if d == 0 else H - depth
        return remote(
            buf.at[pl.ds(src_x, depth), pl.ds(H, NY)],
            buf.at[pl.ds(dst_x, depth), pl.ds(H, NY)],
            xs.at[e, d],
            xr.at[e, d],
            at(x=x_gx[d]),
        )

    def relay(e, side, j, d):
        buf = ref_of(e)
        depth = (8 if e < 2 else 6) - 2 * j
        y0 = jnp.where(y_right[side], H + NY + 2 * (j - 1), H - 2 * j)
        src_x = H if d == 0 else H + NX - depth
        dst_x = H + NX if d == 0 else H - depth
        return remote(
            buf.at[pl.ds(src_x, depth), pl.ds(y0, 2)],
            buf.at[pl.ds(dst_x, depth), pl.ds(y0, 2)],
            rs.at[e, side, j - 1, d],
            rr.at[e, side, j - 1, d],
            at(x=x_gx[d]),
        )

    def reach(e):
        return 4 if e < 2 else 3

    def send_y(e, side):
        @when_side(side)
        def _():
            for j in range(1, reach(e) + 1):
                y_copy(e, side, j).start()

    def send_x(e):
        for d in range(2):
            pl.when(x_there[d])(lambda d=d: x_copy(e, d).start())

    def pass_on(e, side, j):
        @when_side(side)
        def _():
            y_copy(e, side, j).wait_recv()

        if j < reach(e):
            for d in range(2):
                when_side(side, x_there[d])(lambda d=d: relay(e, side, j, d).start())

    def finish(e):
        for d in range(2):

            @pl.when(x_there[d])
            def _(d=d):
                x_copy(e, 1 - d).wait_recv()

            for side in range(2):

                @when_side(side, x_there[d])
                def _(d=d, side=side):
                    for j in range(1, reach(e)):
                        relay(e, side, j, 1 - d).wait_recv()

    def drain(e):
        for side in range(2):

            @when_side(side)
            def _(side=side):
                for j in range(1, reach(e) + 1):
                    y_copy(e, side, j).wait_send()

            for d in range(2):

                @when_side(side, x_there[d])
                def _(side=side, d=d):
                    for j in range(1, reach(e)):
                        relay(e, side, j, d).wait_send()

        for d in range(2):
            pl.when(x_there[d])(lambda d=d: x_copy(e, d).wait_send())

    def band_copy(t, i):
        return remote(
            D.at[t, band], D.at[t, band], bs.at[t, i - 1], br.at[t, i - 1], at(b=lax.rem(band + i, n_band))
        )

    def band_from(t, i):
        other = lax.rem(band + n_band - i, n_band)
        return remote(D.at[t, other], D.at[t, other], bs.at[t, i - 1], br.at[t, i - 1], at(b=other))

    lane = lax.broadcasted_iota(jnp.int32, (F, NZ), 1)
    back_1 = jnp.where(lane >= 1, near_w, 0.0)
    on_1 = jnp.where(lane < NZ - 1, near_w, 0.0)
    back_2 = jnp.where(lane >= 2, far_w, 0.0)
    on_2 = jnp.where(lane < NZ - 2, far_w, 0.0)

    def block(t, src, dst, x0, y0):
        u = {}
        for dx in range(-2, 4):
            for dy in range(-2, 6):
                if 0 <= dx < 2 or 0 <= dy < 4:
                    u[dx, dy] = S[src, x0 + dx, y0 + dy]
        for dx in range(2):
            for dy in range(4):
                c = u[dx, dy]
                one = (u[dx - 1, dy] + u[dx + 1, dy]) + (u[dx, dy - 1] + u[dx, dy + 1])
                two = (u[dx - 2, dy] + u[dx + 2, dy]) + (u[dx, dy - 2] + u[dx, dy + 2])
                along = (back_1 * pltpu.roll(c, 1, 1) + on_1 * pltpu.roll(c, NZ - 1, 1)) + (
                    back_2 * pltpu.roll(c, 2, 1) + on_2 * pltpu.roll(c, NZ - 2, 1)
                )
                S[dst, x0 + dx, y0 + dy] = (V[t, x0 + dx, y0 + dy] * c + near_w * one) + (far_w * two + along)

    def applications(t):
        def step(k, carry):
            r = 4 - k
            src = jnp.where(k == 1, t, k)

            def over_x(xp, carry):
                dx = jnp.maximum(jnp.maximum(4 - xp, xp - 7), 0)
                low = jnp.where(gy == 0, 4, 4 - (r - dx))
                high = jnp.where(gy == n_gy - 1, 10, 10 + (r - dx))

                def over_y(i, carry):
                    block(t, src, k + 1, 2 * xp, 2 * jnp.minimum(low + 2 * i, high - 2))
                    return carry

                return lax.fori_loop(0, lax.div(high - low + 1, 2), over_y, carry)

            first = jnp.where(gx == 0, 4, 4 - r)
            last = jnp.where(gx == n_gx - 1, 8, 8 + r)
            return lax.fori_loop(first, last, over_x, carry)

        lax.fori_loop(1, 5, step, 0)

    sub = lax.broadcasted_iota(jnp.int32, (F, NZ), 0)
    sign = jnp.where(sub < F // 2, 1.0, -1.0)

    def combine(s, w):
        even = w[0] + ((s**4 / 24.0) * w[4] - (s**2 / 2.0) * w[2])
        odd_part = s * w[1] - (s**3 / 6.0) * w[3]
        return even + sign * pltpu.roll(odd_part, F // 2, 0)

    def terms(t, x, y):
        return [S[t, H + x, H + y]] + [S[k, H + x, H + y] for k in range(2, 6)]

    def phase(t):
        send_y(t, 1)
        send_y(t, 0)
        for i in range(1, n_band):
            band_copy(t, i).start()
        send_x(t)
        for i in range(1, n_band):
            band_from(t, i).wait_recv()

        def to_potential(x, y):
            total = (D[t, 0, x, y] + D[t, 1, x, y]) + (D[t, 2, x, y] + D[t, 3, x, y])
            v = ext[pl.ds(x * NY + y, 1), :] - exchange_coef * cube_root(total)
            if t == 1:
                pot[pl.ds(x * NY + y, 1), :] = v
            V[t, H + x, H + y] = v + centre

        own_cells(to_potential, 4)
        send_y(t + 2, 1)
        send_y(t + 2, 0)
        send_x(t + 2)
        for j in range(1, 5):
            pass_on(t, 0, j)
        for j in range(1, 4):
            pass_on(t + 2, 0, j)
        for j in range(1, 5):
            pass_on(t, 1, j)
        for j in range(1, 4):
            pass_on(t + 2, 1, j)
        finish(t)
        finish(t + 2)
        applications(t)

    phase(0)

    def half_way(x, y):
        w = terms(0, x, y)
        D[1, band, x, y] = density_of(combine(step_length, w))
        S[1, H + x, H + y] = combine(step_length / 2, w)

    own_cells(half_way, 2)
    phase(1)

    def take_out(x, y):
        out[pl.ds(x * NY + y, F, stride=NX * NY), :] = combine(step_length / 2, terms(1, x, y))

    own_cells(take_out, 2)
    for t in range(2):
        for i in range(1, n_band):
            band_copy(t, i).wait_send()
        drain(t)
        drain(t + 2)


def body(orbitals, external):
    rows = NX * NY
    vmem = pl.BlockSpec(memory_space=pltpu.VMEM)
    dma = pltpu.SemaphoreType.DMA
    out, pot = pl.pallas_call(
        kernel,
        out_shape=(
            jax.ShapeDtypeStruct((F * rows, NZ), jnp.float32),
            jax.ShapeDtypeStruct((rows, NZ), jnp.float32),
        ),
        in_specs=[vmem, vmem],
        out_specs=(vmem, vmem),
        scratch_shapes=[
            pltpu.VMEM((6, EX, EY, F, NZ), jnp.float32),
            pltpu.VMEM((2, EX, EY, 1, NZ), jnp.float32),
            pltpu.VMEM((2, 4, NX, NY, 1, NZ), jnp.float32),
            dma((4, 2, 4)),
            dma((4, 2, 4)),
            dma((4, 2)),
            dma((4, 2)),
            dma((4, 2, 3, 2)),
            dma((4, 2, 3, 2)),
            dma((2, 3)),
            dma((2, 3)),
        ],
        compiler_params=pltpu.CompilerParams(
            collective_id=0, has_side_effects=True, vmem_limit_bytes=40 * 1024 * 1024
        ),
        name="etrs",
    )(orbitals.reshape(F * rows, NZ), external.reshape(rows, NZ))
    return out.reshape(orbitals.shape), pot.reshape(external.shape)


def solution(mesh):
    in_specs = (P(None, "band", "gx", "gy", None), P("gx", "gy", None))
    out_specs = (P(None, "band", "gx", "gy", None), P("gx", "gy", None))
    return jax.shard_map(body, mesh=mesh, in_specs=in_specs, out_specs=out_specs, check_vma=False)
```

time: 239 us -> 129 us (0.54)
  the two profiles are of different devices: /device:TPU:103 before, /device:TPU:76 now
where the time goes in v1:
time: 129 us
  Pallas kernels  125 us (97%)
  local copies, waits for them, and re-layouts  3.48 us (3%)
    pallas_call x1, Pallas kernels, body(): pl.pallas_call(kernel, out_shape=(jax.ShapeDtypeStruct((F * rows, NZ), jn...  125 us
    unnamed x4, local copies, waits for them, and re-layouts  3.39 us

profile of v1, /device:TPU:76, one launch (start us, length us, event | category | flops | bytes accessed | tf_op | source)
XLA Modules:
  0.0 128.8 jit_solution(7923039332503536735)
XLA Ops:
  0.6 0.8 copy.9
  1.5 1.1 copy.8
  2.6 124.6 %etrs.1 = (f32[768,128]{1,0:T(8,128)S(1)}, f32[96,128]{1,0:T(8,128)S(1)}) custom-call(f32[768,128]{1,0:T(8,128)S(1)} %reshape.16.orb, f32[96,128]{1,0:T(8,128)S(1)} %reshape.17.ext), custom_call_target="tpu_custom_call" | custom-call | tf_op jit(solution)/shard_map/etrs/pallas_call | solution.py:330
  127.2 0.6 copy.11
  127.9 0.9 copy.10
  (4 shorter events, 0.1 us)

commit v2 on v1

--- a/solution.py
+++ b/solution.py
@@ -10,7 +10,6 @@
 step_length = 0.15
 exchange_coef = 0.7386
 centre = 3.75
-near_w = -2.0 / 3.0
 far_w = 1.0 / 24.0
 
 MESH = pl.DeviceIdType.MESH
@@ -27,7 +26,11 @@
     return jnp.where(x > 1e-37, y, 0.0)
 
 
-def kernel(orb, ext, out, pot, S, V, D, ys, yr, xs, xr, rs, rr, bs, br):
+def scope(name):
+    return lambda f: jax.named_scope(name)(f)
+
+
+def kernel(orb, ext, out, pot, S, V, D, Z, ys, yr, xs, xr, rs, rr, bs, br):
     gx, gy, band = lax.axis_index("gx"), lax.axis_index("gy"), lax.axis_index("band")
     n_gx, n_gy, n_band = lax.axis_size("gx"), lax.axis_size("gy"), lax.axis_size("band")
     odd = lax.rem(gy, 2)
@@ -103,15 +106,32 @@
     pl.when(gy == 0)(lambda: clear_y(H - 2))
     pl.when(gy == n_gy - 1)(lambda: clear_y(H + NY))
 
-    pl.semaphore_wait(bar, count)
+    off = jnp.abs(lax.broadcasted_iota(jnp.int32, (NZ, NZ), 0) - lax.broadcasted_iota(jnp.int32, (NZ, NZ), 1))
+    z_part = jnp.where(off == 1, -16.0, jnp.where(off == 2, 1.0, 0.0)).astype(jnp.bfloat16)
+    Z[0:NZ, :] = z_part
+    Z[NZ:, :] = z_part
+
+    with jax.named_scope('barrier'):
+        pl.semaphore_wait(bar, count)
 
     def remote(src, dst, s, r, dev):
         return pltpu.make_async_remote_copy(
             src_ref=src, dst_ref=dst, send_sem=s, recv_sem=r, device_id=dev, device_id_type=MESH
         )
 
+    def remote(src, dst, s, r, dev):
+        return pltpu.make_async_remote_copy(
+            src_ref=src, dst_ref=dst, send_sem=s, recv_sem=r, device_id=dev, device_id_type=MESH
+        )
+
+    def row_of(pair):
+        return jnp.where(odd == 1, H + NY - 2 - 2 * pair, H + 2 * pair)
+
     def ref_of(e):
         return S.at[e] if e < 2 else V.at[e - 2]
+
+    def reach(e):
+        return 4 if e < 2 else 3
 
     def y_copy(e, side, j):
         buf = ref_of(e)
@@ -125,22 +145,23 @@
             at(y=y_gy[side]),
         )
 
-    def x_copy(e, d):
+    def x_copy(e, pair, d):
         buf = ref_of(e)
-        depth = 8 if e < 2 else 6
+        depth = 2 * reach(e)
+        rows = pl.ds(row_of(pair), 2) if e < 2 else pl.ds(H, NY)
         src_x = H if d == 0 else H + NX - depth
         dst_x = H + NX if d == 0 else H - depth
         return remote(
-            buf.at[pl.ds(src_x, depth), pl.ds(H, NY)],
-            buf.at[pl.ds(dst_x, depth), pl.ds(H, NY)],
-            xs.at[e, d],
-            xr.at[e, d],
+            buf.at[pl.ds(src_x, depth), rows],
+            buf.at[pl.ds(dst_x, depth), rows],
+            xs.at[e, pair, d],
+            xr.at[e, pair, d],
             at(x=x_gx[d]),
         )
 
     def relay(e, side, j, d):
         buf = ref_of(e)
-        depth = (8 if e < 2 else 6) - 2 * j
+        depth = 2 * (reach(e) - j)
         y0 = jnp.where(y_right[side], H + NY + 2 * (j - 1), H - 2 * j)
         src_x = H if d == 0 else H + NX - depth
         dst_x = H + NX if d == 0 else H - depth
@@ -152,41 +173,49 @@
             at(x=x_gx[d]),
         )
 
-    def reach(e):
-        return 4 if e < 2 else 3
-
-    def send_y(e, side):
+    def send_y(e, side, pieces):
         @when_side(side)
         def _():
-            for j in range(1, reach(e) + 1):
+            for j in pieces:
                 y_copy(e, side, j).start()
 
-    def send_x(e):
-        for d in range(2):
-            pl.when(x_there[d])(lambda d=d: x_copy(e, d).start())
-
-    def pass_on(e, side, j):
-        @when_side(side)
-        def _():
-            y_copy(e, side, j).wait_recv()
-
-        if j < reach(e):
-            for d in range(2):
-                when_side(side, x_there[d])(lambda d=d: relay(e, side, j, d).start())
-
-    def finish(e):
+    def x_pairs(e):
+        return range(NY // 2) if e < 2 else range(1)
+
+    def send_x(e, pairs):
         for d in range(2):
 
             @pl.when(x_there[d])
             def _(d=d):
-                x_copy(e, 1 - d).wait_recv()
-
-            for side in range(2):
-
-                @when_side(side, x_there[d])
-                def _(d=d, side=side):
-                    for j in range(1, reach(e)):
-                        relay(e, side, j, 1 - d).wait_recv()
+                for pair in pairs:
+                    x_copy(e, pair, d).start()
+
+    def pass_on(e, side, pieces):
+        for j in pieces:
+
+            @when_side(side)
+            def _(j=j):
+                y_copy(e, side, j).wait_recv()
+
+            if j < reach(e):
+                for d in range(2):
+                    when_side(side, x_there[d])(lambda j=j, d=d: relay(e, side, j, d).start())
+
+    def await_relay(e, side, pieces):
+        for d in range(2):
+
+            @when_side(side, x_there[d])
+            def _(d=d):
+                for j in pieces:
+                    relay(e, side, j, 1 - d).wait_recv()
+
+    def await_x(e):
+        for d in range(2):
+
+            @pl.when(x_there[d])
+            def _(d=d):
+                for pair in x_pairs(e):
+                    x_copy(e, pair, 1 - d).wait_recv()
 
     def drain(e):
         for side in range(2):
@@ -204,7 +233,11 @@
                         relay(e, side, j, d).wait_send()
 
         for d in range(2):
-            pl.when(x_there[d])(lambda d=d: x_copy(e, d).wait_send())
+
+            @pl.when(x_there[d])
+            def _(d=d):
+                for pair in x_pairs(e):
+                    x_copy(e, pair, d).wait_send()
 
     def band_copy(t, i):
         return remote(
@@ -215,49 +248,54 @@
         other = lax.rem(band + n_band - i, n_band)
         return remote(D.at[t, other], D.at[t, other], bs.at[t, i - 1], br.at[t, i - 1], at(b=other))
 
-    lane = lax.broadcasted_iota(jnp.int32, (F, NZ), 1)
-    back_1 = jnp.where(lane >= 1, near_w, 0.0)
-    on_1 = jnp.where(lane < NZ - 1, near_w, 0.0)
-    back_2 = jnp.where(lane >= 2, far_w, 0.0)
-    on_2 = jnp.where(lane < NZ - 2, far_w, 0.0)
-
-    def block(t, src, dst, x0, y0):
+    def unit(t, k, pair, width):
+        src, dst = (t if k == 1 else k), k + 1
+        y0, x0 = row_of(pair), H + NX // 2 - width // 2
         u = {}
-        for dx in range(-2, 4):
-            for dy in range(-2, 6):
-                if 0 <= dx < 2 or 0 <= dy < 4:
+        for dx in range(-2, width + 2):
+            for dy in range(-2, 4):
+                if 0 <= dx < width or 0 <= dy < 2:
                     u[dx, dy] = S[src, x0 + dx, y0 + dy]
-        for dx in range(2):
-            for dy in range(4):
-                c = u[dx, dy]
+        stack = jnp.concatenate([u[dx, dy] for dx in range(width) for dy in range(2)], axis=0)
+        high = stack.astype(jnp.bfloat16)
+        low = (stack - high.astype(jnp.float32)).astype(jnp.bfloat16)
+        along = jnp.dot(
+            jnp.concatenate([high, low], axis=1), Z[...], preferred_element_type=jnp.float32
+        )
+        for dx in range(width):
+            for dy in range(2):
                 one = (u[dx - 1, dy] + u[dx + 1, dy]) + (u[dx, dy - 1] + u[dx, dy + 1])
                 two = (u[dx - 2, dy] + u[dx + 2, dy]) + (u[dx, dy - 2] + u[dx, dy + 2])
-                along = (back_1 * pltpu.roll(c, 1, 1) + on_1 * pltpu.roll(c, NZ - 1, 1)) + (
-                    back_2 * pltpu.roll(c, 2, 1) + on_2 * pltpu.roll(c, NZ - 2, 1)
-                )
-                S[dst, x0 + dx, y0 + dy] = (V[t, x0 + dx, y0 + dy] * c + near_w * one) + (far_w * two + along)
-
-    def applications(t):
-        def step(k, carry):
-            r = 4 - k
-            src = jnp.where(k == 1, t, k)
-
-            def over_x(xp, carry):
-                dx = jnp.maximum(jnp.maximum(4 - xp, xp - 7), 0)
-                low = jnp.where(gy == 0, 4, 4 - (r - dx))
-                high = jnp.where(gy == n_gy - 1, 10, 10 + (r - dx))
-
-                def over_y(i, carry):
-                    block(t, src, k + 1, 2 * xp, 2 * jnp.minimum(low + 2 * i, high - 2))
+                at_cell = F * (2 * dx + dy)
+                around = (two + along[at_cell : at_cell + F]) - 16.0 * one
+                S[dst, x0 + dx, y0 + dy] = V[t, x0 + dx, y0 + dy] * u[dx, dy] + far_w * around
+        if width > NX:
+            for d, edge in ((0, H - 2), (1, H + NX)):
+
+                @pl.when(jnp.logical_not(x_there[d]))
+                def _(edge=edge):
+                    for dx in range(2):
+                        for dy in range(2):
+                            S[dst, edge + dx, y0 + dy] = zero
+
+    def stage(t, j):
+        if j == 0:
+            for k in range(1, 5):
+
+                def one_pair(pair, carry, k=k):
+                    unit(t, k, pair, NX + 4 * (4 - k))
                     return carry
 
-                return lax.fori_loop(0, lax.div(high - low + 1, 2), over_y, carry)
-
-            first = jnp.where(gx == 0, 4, 4 - r)
-            last = jnp.where(gx == n_gx - 1, 8, 8 + r)
-            return lax.fori_loop(first, last, over_x, carry)
-
-        lax.fori_loop(1, 5, step, 0)
+                lax.fori_loop(k, 10 - k, one_pair, 0)
+            return
+
+        def some(ks):
+            for k in ks:
+                unit(t, k, k - j, NX + 4 * (4 - k - max(j - k, 0)))
+
+        if j > 1:
+            pl.when(far_there)(lambda: some(range(1, j)))
+        some(range(j, 5))
 
     sub = lax.broadcasted_iota(jnp.int32, (F, NZ), 0)
     sign = jnp.where(sub < F // 2, 1.0, -1.0)
@@ -267,60 +305,135 @@
         odd_part = s * w[1] - (s**3 / 6.0) * w[3]
         return even + sign * pltpu.roll(odd_part, F // 2, 0)
 
+    def each_of(pair, body):
+        y0 = row_of(pair)
+
+        def step(i, carry):
+            for dx in range(4):
+                for dy in range(2):
+                    body(4 * i + dx, y0 - H + dy)
+            return carry
+
+        lax.fori_loop(0, NX // 4, step, 0)
+
     def terms(t, x, y):
         return [S[t, H + x, H + y]] + [S[k, H + x, H + y] for k in range(2, 6)]
 
-    def phase(t):
-        send_y(t, 1)
-        send_y(t, 0)
-        for i in range(1, n_band):
-            band_copy(t, i).start()
-        send_x(t)
-        for i in range(1, n_band):
-            band_from(t, i).wait_recv()
-
-        def to_potential(x, y):
+    def half_way(x, y):
+        w = terms(0, x, y)
+        D[1, band, x, y] = density_of(combine(step_length, w))
+        S[1, H + x, H + y] = combine(step_length / 2, w)
+
+    def half_row(pair):
+        each_of(pair, half_way)
+        if pair < 4:
+            send_y(1, 1, [pair + 1])
+        if pair > 1:
+            send_y(1, 0, [6 - pair])
+        send_x(1, [pair])
+
+    def take_out(x, y):
+        out[pl.ds(x * NY + y, F, stride=NX * NY), :] = combine(step_length / 2, terms(1, x, y))
+
+    def out_row(pair):
+        each_of(pair, take_out)
+
+    def to_potential(t):
+        def cell(x, y):
             total = (D[t, 0, x, y] + D[t, 1, x, y]) + (D[t, 2, x, y] + D[t, 3, x, y])
             v = ext[pl.ds(x * NY + y, 1), :] - exchange_coef * cube_root(total)
             if t == 1:
                 pot[pl.ds(x * NY + y, 1), :] = v
             V[t, H + x, H + y] = v + centre
 
-        own_cells(to_potential, 4)
-        send_y(t + 2, 1)
-        send_y(t + 2, 0)
-        send_x(t + 2)
+        own_cells(cell, 4)
+
+    def sum_over_band(t):
+        for i in range(1, n_band):
+            band_from(t, i).wait_recv()
+
+    U, W = range(1, 5), range(1, 4)
+
+    for i in range(1, n_band):
+        band_copy(0, i).start()
+    send_y(0, 1, [1, 2])
+    send_y(0, 0, U)
+    send_x(0, x_pairs(0))
+    scope('band0')(sum_over_band)(0)
+    scope('pot0')(to_potential)(0)
+    send_y(2, 1, W)
+    send_y(2, 0, W)
+    send_x(2, x_pairs(2))
+    send_y(0, 1, [3, 4])
+    with jax.named_scope('near0'):
+        pass_on(0, 0, U)
+        pass_on(2, 0, W)
+    with jax.named_scope('x0'):
+        await_x(0)
+        await_x(2)
+    with jax.named_scope('nearrelay0'):
+        await_relay(0, 0, W)
+        await_relay(2, 0, [1, 2])
+    with jax.named_scope('stage00'):
+        stage(0, 0)
+    with jax.named_scope('half00'):
+        half_row(5)
+        half_row(4)
+    with jax.named_scope('far01'):
+        pass_on(0, 1, [1])
+    for j in range(1, 5):
+        if j < 4:
+            with jax.named_scope(f'farU0{j+1}'):
+                pass_on(0, 1, [j + 1])
+            with jax.named_scope(f'farV0{j}'):
+                pass_on(2, 1, [j])
+            with jax.named_scope(f'farrelay0{j}'):
+                await_relay(0, 1, [j])
+                if j > 1:
+                    await_relay(2, 1, [j - 1])
+        with jax.named_scope(f'stage0{j}'):
+            stage(0, j)
+        with jax.named_scope(f'half0{j}'):
+            half_row(4 - j)
+
+    for i in range(1, n_band):
+        band_copy(1, i).start()
+    with jax.named_scope('near1'):
+        pass_on(1, 0, U)
+    scope('band1')(sum_over_band)(1)
+    scope('pot1')(to_potential)(1)
+    send_y(3, 1, W)
+    send_y(3, 0, W)
+    send_x(3, x_pairs(3))
+    with jax.named_scope('nearV1'):
+        pass_on(3, 0, W)
+    with jax.named_scope('x1'):
+        await_x(1)
+        await_x(3)
+    with jax.named_scope('nearrelay1'):
+        await_relay(1, 0, W)
+        await_relay(3, 0, [1, 2])
+    with jax.named_scope('stage10'):
+        stage(1, 0)
+        out_row(5)
+        out_row(4)
+    with jax.named_scope('farU1'):
+        pass_on(1, 1, [4, 3, 2, 1])
+    with jax.named_scope('farV1'):
+        pass_on(3, 1, W)
+    with jax.named_scope('farrelay1'):
+        await_relay(1, 1, W)
+        await_relay(3, 1, [1, 2])
+    with jax.named_scope('stages1'):
         for j in range(1, 5):
-            pass_on(t, 0, j)
-        for j in range(1, 4):
-            pass_on(t + 2, 0, j)
-        for j in range(1, 5):
-            pass_on(t, 1, j)
-        for j in range(1, 4):
-            pass_on(t + 2, 1, j)
-        finish(t)
-        finish(t + 2)
-        applications(t)
-
-    phase(0)
-
-    def half_way(x, y):
-        w = terms(0, x, y)
-        D[1, band, x, y] = density_of(combine(step_length, w))
-        S[1, H + x, H + y] = combine(step_length / 2, w)
-
-    own_cells(half_way, 2)
-    phase(1)
-
-    def take_out(x, y):
-        out[pl.ds(x * NY + y, F, stride=NX * NY), :] = combine(step_length / 2, terms(1, x, y))
-
-    own_cells(take_out, 2)
-    for t in range(2):
-        for i in range(1, n_band):
-            band_copy(t, i).wait_send()
-        drain(t)
-        drain(t + 2)
+            stage(1, j)
+            out_row(4 - j)
+    with jax.named_scope('drain'):
+        for t in range(2):
+            for i in range(1, n_band):
+                band_copy(t, i).wait_send()
+            drain(t)
+            drain(t + 2)
 
 
 def body(orbitals, external):
@@ -339,10 +452,11 @@
             pltpu.VMEM((6, EX, EY, F, NZ), jnp.float32),
             pltpu.VMEM((2, EX, EY, 1, NZ), jnp.float32),
             pltpu.VMEM((2, 4, NX, NY, 1, NZ), jnp.float32),
+            pltpu.VMEM((2 * NZ, NZ), jnp.bfloat16),
             dma((4, 2, 4)),
             dma((4, 2, 4)),
-            dma((4, 2)),
-            dma((4, 2)),
+            dma((4, 6, 2)),
+            dma((4, 6, 2)),
             dma((4, 2, 3, 2)),
             dma((4, 2, 3, 2)),
             dma((2, 3)),

time: 129 us -> 116 us (0.90)
  the two profiles are of different devices: /device:TPU:76 before, /device:TPU:58 now
where the time goes in v2:
time: 116 us
  Pallas kernels  112 us (97%)
  local copies, waits for them, and re-layouts  3.48 us (3%)
    pallas_call x1, Pallas kernels, body(): pl.pallas_call(kernel, out_shape=(jax.ShapeDtypeStruct((F * rows, NZ), jn...  112 us
    unnamed x4, local copies, waits for them, and re-layouts  3.39 us

profile of v2, /device:TPU:58, one launch (start us, length us, event | category | flops | bytes accessed | tf_op | source)
XLA Modules:
  0.0 116.0 jit_solution(10621096586675230499)
XLA Ops:
  0.6 0.8 copy.9
  1.5 1.1 copy.8
  2.6 111.8 %etrs.1 = (f32[768,128]{1,0:T(8,128)S(1)}, f32[96,128]{1,0:T(8,128)S(1)}) custom-call(f32[768,128]{1,0:T(8,128)S(1)} %reshape.16.orb, f32[96,128]{1,0:T(8,128)S(1)} %reshape.17.ext), custom_call_target="tpu_custom_call" | custom-call | tf_op jit(solution)/shard_map/etrs/pallas_call | solution.py:443
  114.4 0.6 copy.11
  115.1 0.9 copy.10
  (4 shorter events, 0.1 us)

commit v3 on v2

--- a/solution.py
+++ b/solution.py
@@ -26,11 +26,7 @@
     return jnp.where(x > 1e-37, y, 0.0)
 
 
-def scope(name):
-    return lambda f: jax.named_scope(name)(f)
-
-
-def kernel(orb, ext, out, pot, S, V, D, Z, ys, yr, xs, xr, rs, rr, bs, br):
+def kernel(orb_in, ext_in, out, pot, S, V, D, Z, orb, ext, ys, yr, xs, xr, rs, rr, bs, br, vs, vr, ins):
     gx, gy, band = lax.axis_index("gx"), lax.axis_index("gy"), lax.axis_index("band")
     n_gx, n_gy, n_band = lax.axis_size("gx"), lax.axis_size("gy"), lax.axis_size("band")
     odd = lax.rem(gy, 2)
@@ -63,6 +59,10 @@
         greet(at(b=lax.rem(band + i, n_band)))
     greet(at(y=y_gy[0]))
 
+    fetch = [pltpu.make_async_copy(a, b, ins.at[i]) for i, (a, b) in enumerate(((orb_in, orb), (ext_in, ext)))]
+    for copy in fetch:
+        copy.start()
+
     def density_of(u):
         return jnp.sum(u * u, axis=0, keepdims=True)
 
@@ -75,10 +75,17 @@
         lax.fori_loop(0, NX * (NY // unroll), step, 0)
 
     def take_in(x, y):
-        u = orb[pl.ds(x * NY + y, F, stride=NX * NY), :]
+        u = orb[pl.ds(y * NX + x, F, stride=NX * NY), :]
         S[0, H + x, H + y] = u
         D[0, band, x, y] = density_of(u)
 
+    off = jnp.abs(lax.broadcasted_iota(jnp.int32, (NZ, NZ), 0) - lax.broadcasted_iota(jnp.int32, (NZ, NZ), 1))
+    z_part = jnp.where(off == 1, -16.0, jnp.where(off == 2, 1.0, 0.0)).astype(jnp.bfloat16)
+    Z[0:NZ, :] = z_part
+    Z[NZ:, :] = z_part
+
+    for copy in fetch:
+        copy.wait()
     own_cells(take_in, 4)
 
     zero = jnp.zeros((F, NZ), jnp.float32)
@@ -106,18 +113,8 @@
     pl.when(gy == 0)(lambda: clear_y(H - 2))
     pl.when(gy == n_gy - 1)(lambda: clear_y(H + NY))
 
-    off = jnp.abs(lax.broadcasted_iota(jnp.int32, (NZ, NZ), 0) - lax.broadcasted_iota(jnp.int32, (NZ, NZ), 1))
-    z_part = jnp.where(off == 1, -16.0, jnp.where(off == 2, 1.0, 0.0)).astype(jnp.bfloat16)
-    Z[0:NZ, :] = z_part
-    Z[NZ:, :] = z_part
-
     with jax.named_scope('barrier'):
         pl.semaphore_wait(bar, count)
-
-    def remote(src, dst, s, r, dev):
-        return pltpu.make_async_remote_copy(
-            src_ref=src, dst_ref=dst, send_sem=s, recv_sem=r, device_id=dev, device_id_type=MESH
-        )
 
     def remote(src, dst, s, r, dev):
         return pltpu.make_async_remote_copy(
@@ -148,7 +145,7 @@
     def x_copy(e, pair, d):
         buf = ref_of(e)
         depth = 2 * reach(e)
-        rows = pl.ds(row_of(pair), 2) if e < 2 else pl.ds(H, NY)
+        rows = pl.ds(row_of(pair), 2)
         src_x = H if d == 0 else H + NX - depth
         dst_x = H + NX if d == 0 else H - depth
         return remote(
@@ -162,15 +159,22 @@
     def relay(e, side, j, d):
         buf = ref_of(e)
         depth = 2 * (reach(e) - j)
-        y0 = jnp.where(y_right[side], H + NY + 2 * (j - 1), H - 2 * j)
-        src_x = H if d == 0 else H + NX - depth
-        dst_x = H + NX if d == 0 else H - depth
+        src_y = jnp.where(y_right[side], H + NY - 2 * j, H + 2 * (j - 1))
+        dst_y = jnp.where(y_right[side], H - 2 * j, H + NY + 2 * (j - 1))
+        if side == 0:
+            dst_x = H - depth if d == 0 else H + NX
+            src_x, dev = dst_x, at(y=y_gy[0])
+        else:
+            dst_y = src_y = jnp.where(y_right[1], H + NY + 2 * (j - 1), H - 2 * j)
+            src_x = H if d == 0 else H + NX - depth
+            dst_x = H + NX if d == 0 else H - depth
+            dev = at(x=x_gx[d])
         return remote(
-            buf.at[pl.ds(src_x, depth), pl.ds(y0, 2)],
-            buf.at[pl.ds(dst_x, depth), pl.ds(y0, 2)],
+            buf.at[pl.ds(src_x, depth), pl.ds(src_y, 2)],
+            buf.at[pl.ds(dst_x, depth), pl.ds(dst_y, 2)],
             rs.at[e, side, j - 1, d],
             rr.at[e, side, j - 1, d],
-            at(x=x_gx[d]),
+            dev,
         )
 
     def send_y(e, side, pieces):
@@ -179,9 +183,6 @@
             for j in pieces:
                 y_copy(e, side, j).start()
 
-    def x_pairs(e):
-        return range(NY // 2) if e < 2 else range(1)
-
     def send_x(e, pairs):
         for d in range(2):
 
@@ -190,16 +191,39 @@
                 for pair in pairs:
                     x_copy(e, pair, d).start()
 
-    def pass_on(e, side, pieces):
+    def take_far(e, pieces):
+        @when_side(1)
+        def _():
+            for j in pieces:
+                y_copy(e, 1, j).wait_recv()
+                if j < reach(e):
+                    for d in range(2):
+                        pl.when(x_there[d])(lambda j=j, d=d: relay(e, 1, j, d).start())
+
+    def spread(j, i):
+        part = V.at[0, pl.ds(H, NX), pl.ds(row_of(-j), 2)]
+        return remote(part, part, vs.at[j - 1, i - 1], vr.at[j - 1], at(b=lax.rem(band + i, n_band)))
+
+    def take_far_potential(pieces):
         for j in pieces:
 
-            @when_side(side)
+            @pl.when(far_there & (band == j - 1))
             def _(j=j):
-                y_copy(e, side, j).wait_recv()
-
-            if j < reach(e):
+                y_copy(2, 1, j).wait_recv()
+                for i in range(1, n_band):
+                    spread(j, i).start()
+
+            @pl.when(far_there & (band != j - 1))
+            def _(j=j):
+                spread(j, 1).wait_recv()
+
+            if j < 3:
                 for d in range(2):
-                    when_side(side, x_there[d])(lambda j=j, d=d: relay(e, side, j, d).start())
+                    when_side(1, x_there[d])(lambda j=j, d=d: relay(2, 1, j, d).start())
+
+    def await_near(e):
+        for j in range(1, reach(e) + 1):
+            y_copy(e, 0, j).wait_recv()
 
     def await_relay(e, side, pieces):
         for d in range(2):
@@ -207,23 +231,32 @@
             @when_side(side, x_there[d])
             def _(d=d):
                 for j in pieces:
-                    relay(e, side, j, 1 - d).wait_recv()
-
-    def await_x(e):
+                    relay(e, side, j, 1 - d if side else d).wait_recv()
+
+    def await_x(e, pairs):
         for d in range(2):
 
             @pl.when(x_there[d])
             def _(d=d):
-                for pair in x_pairs(e):
+                for pair in pairs:
                     x_copy(e, pair, 1 - d).wait_recv()
+                    j = NY // 2 - pair
+                    if j < reach(e):
+                        relay(e, 0, j, d).start()
 
     def drain(e):
         for side in range(2):
 
-            @when_side(side)
-            def _(side=side):
-                for j in range(1, reach(e) + 1):
-                    y_copy(e, side, j).wait_send()
+            for j in range(1, reach(e) + 1):
+                if side == 0 or e != 2:
+                    when_side(side)(lambda j=j, side=side: y_copy(e, side, j).wait_send())
+                else:
+
+                    @pl.when(far_there & (band == j - 1))
+                    def _(j=j):
+                        y_copy(e, 1, j).wait_send()
+                        for i in range(1, n_band):
+                            spread(j, i).wait_send()
 
             for d in range(2):
 
@@ -236,17 +269,24 @@
 
             @pl.when(x_there[d])
             def _(d=d):
-                for pair in x_pairs(e):
+                for pair in range(NY // 2):
                     x_copy(e, pair, d).wait_send()
 
-    def band_copy(t, i):
-        return remote(
-            D.at[t, band], D.at[t, band], bs.at[t, i - 1], br.at[t, i - 1], at(b=lax.rem(band + i, n_band))
-        )
-
-    def band_from(t, i):
+    def band_rows(t, whose, pair):
+        return D.at[t, whose, pl.ds(0, NX), pl.ds(row_of(pair) - H, 2)]
+
+    def band_copy(t, pair, i):
+        part = band_rows(t, band, pair)
+        return remote(part, part, bs.at[t, pair, i - 1], br.at[t, pair, i - 1], at(b=lax.rem(band + i, n_band)))
+
+    def band_from(t, pair, i):
         other = lax.rem(band + n_band - i, n_band)
-        return remote(D.at[t, other], D.at[t, other], bs.at[t, i - 1], br.at[t, i - 1], at(b=other))
+        part = band_rows(t, other, pair)
+        return remote(part, part, bs.at[t, pair, i - 1], br.at[t, pair, i - 1], at(b=other))
+
+    def send_band(t, pair):
+        for i in range(1, n_band):
+            band_copy(t, pair, i).start()
 
     def unit(t, k, pair, width):
         src, dst = (t if k == 1 else k), k + 1
@@ -326,112 +366,121 @@
 
     def half_row(pair):
         each_of(pair, half_way)
-        if pair < 4:
+        send_band(1, pair)
+        if 0 < pair < 4:
             send_y(1, 1, [pair + 1])
         if pair > 1:
             send_y(1, 0, [6 - pair])
         send_x(1, [pair])
 
     def take_out(x, y):
-        out[pl.ds(x * NY + y, F, stride=NX * NY), :] = combine(step_length / 2, terms(1, x, y))
+        out[pl.ds(y * NX + x, F, stride=NX * NY), :] = combine(step_length / 2, terms(1, x, y))
 
     def out_row(pair):
         each_of(pair, take_out)
 
-    def to_potential(t):
+    def potential_row(t, pair):
+        for i in range(1, n_band):
+            band_from(t, pair, i).wait_recv()
+
         def cell(x, y):
             total = (D[t, 0, x, y] + D[t, 1, x, y]) + (D[t, 2, x, y] + D[t, 3, x, y])
-            v = ext[pl.ds(x * NY + y, 1), :] - exchange_coef * cube_root(total)
+            v = ext[pl.ds(y * NX + x, 1), :] - exchange_coef * cube_root(total)
             if t == 1:
-                pot[pl.ds(x * NY + y, 1), :] = v
+                pot[pl.ds(y * NX + x, 1), :] = v
             V[t, H + x, H + y] = v + centre
 
-        own_cells(cell, 4)
-
-    def sum_over_band(t):
-        for i in range(1, n_band):
-            band_from(t, i).wait_recv()
-
-    U, W = range(1, 5), range(1, 4)
-
-    for i in range(1, n_band):
-        band_copy(0, i).start()
+        each_of(pair, cell)
+        if pair < 3:
+            mine = far_there & (band == pair) if t == 0 else far_there
+            pl.when(mine)(lambda: y_copy(t + 2, 1, pair + 1).start())
+        else:
+            send_y(t + 2, 0, [6 - pair])
+        send_x(t + 2, [pair])
+
+    scope = jax.named_scope
+    rows = range(NY // 2)
+
     send_y(0, 1, [1, 2])
-    send_y(0, 0, U)
-    send_x(0, x_pairs(0))
-    scope('band0')(sum_over_band)(0)
-    scope('pot0')(to_potential)(0)
-    send_y(2, 1, W)
-    send_y(2, 0, W)
-    send_x(2, x_pairs(2))
+    for pair in rows:
+        send_band(0, pair)
+    send_y(0, 0, range(1, 5))
+    send_x(0, rows)
+    with scope('pot0'):
+        for pair in rows:
+            potential_row(0, pair)
     send_y(0, 1, [3, 4])
-    with jax.named_scope('near0'):
-        pass_on(0, 0, U)
-        pass_on(2, 0, W)
-    with jax.named_scope('x0'):
-        await_x(0)
-        await_x(2)
-    with jax.named_scope('nearrelay0'):
-        await_relay(0, 0, W)
+    with scope('far01'):
+        take_far(0, [1])
+    with scope('x0'):
+        await_x(0, rows)
+        await_x(2, rows)
+    with scope('near0'):
+        await_near(0)
+        await_near(2)
+        await_relay(0, 0, [1, 2, 3])
         await_relay(2, 0, [1, 2])
-    with jax.named_scope('stage00'):
+    with scope('stage00'):
         stage(0, 0)
-    with jax.named_scope('half00'):
+    with scope('half00'):
         half_row(5)
         half_row(4)
-    with jax.named_scope('far01'):
-        pass_on(0, 1, [1])
     for j in range(1, 5):
-        if j < 4:
-            with jax.named_scope(f'farU0{j+1}'):
-                pass_on(0, 1, [j + 1])
-            with jax.named_scope(f'farV0{j}'):
-                pass_on(2, 1, [j])
-            with jax.named_scope(f'farrelay0{j}'):
+        with scope(f'far0{j}'):
+            if j < 4:
+                take_far(0, [j + 1])
+                take_far_potential([j])
+        with scope(f'farrelay0{j}'):
+            if j < 4:
                 await_relay(0, 1, [j])
                 if j > 1:
                     await_relay(2, 1, [j - 1])
-        with jax.named_scope(f'stage0{j}'):
+        with scope(f'stage0{j}'):
             stage(0, j)
-        with jax.named_scope(f'half0{j}'):
             half_row(4 - j)
-
-    for i in range(1, n_band):
-        band_copy(1, i).start()
-    with jax.named_scope('near1'):
-        pass_on(1, 0, U)
-    scope('band1')(sum_over_band)(1)
-    scope('pot1')(to_potential)(1)
-    send_y(3, 1, W)
-    send_y(3, 0, W)
-    send_x(3, x_pairs(3))
-    with jax.named_scope('nearV1'):
-        pass_on(3, 0, W)
-    with jax.named_scope('x1'):
-        await_x(1)
-        await_x(3)
-    with jax.named_scope('nearrelay1'):
-        await_relay(1, 0, W)
+        with scope(f'pot1{j}'):
+            if j == 1:
+                potential_row(1, 5)
+                potential_row(1, 4)
+            else:
+                potential_row(1, 5 - j)
+
+    with scope('pot15'):
+        potential_row(1, 0)
+    send_y(1, 1, [1])
+    with scope('far1a'):
+        take_far(1, [4, 3, 2])
+    with scope('x1'):
+        await_x(1, rows)
+        await_x(3, rows)
+    with scope('near1'):
+        await_near(1)
+        await_near(3)
+        await_relay(1, 0, [1, 2, 3])
         await_relay(3, 0, [1, 2])
-    with jax.named_scope('stage10'):
+    with scope('stage10'):
         stage(1, 0)
         out_row(5)
         out_row(4)
-    with jax.named_scope('farU1'):
-        pass_on(1, 1, [4, 3, 2, 1])
-    with jax.named_scope('farV1'):
-        pass_on(3, 1, W)
-    with jax.named_scope('farrelay1'):
-        await_relay(1, 1, W)
+    with scope('farV1'):
+        take_far(3, [3, 2, 1])
+        take_far(1, [1])
+    with scope('farrelay1'):
+        await_relay(1, 1, [1, 2, 3])
+    with scope('stage11'):
+        stage(1, 1)
+        out_row(3)
+    with scope('farrelayV1'):
         await_relay(3, 1, [1, 2])
-    with jax.named_scope('stages1'):
-        for j in range(1, 5):
+    with scope('stages1'):
+        for j in range(2, 5):
             stage(1, j)
             out_row(4 - j)
-    with jax.named_scope('drain'):
+    with scope('drain'):
         for t in range(2):
-            for i in range(1, n_band):
-                band_copy(t, i).wait_send()
+            for pair in rows:
+                for i in range(1, n_band):
+                    band_copy(t, pair, i).wait_send()
             drain(t)
             drain(t + 2)
 
@@ -446,28 +495,37 @@
             jax.ShapeDtypeStruct((F * rows, NZ), jnp.float32),
             jax.ShapeDtypeStruct((rows, NZ), jnp.float32),
         ),
-        in_specs=[vmem, vmem],
+        in_specs=[pl.BlockSpec(memory_space=pltpu.HBM)] * 2,
         out_specs=(vmem, vmem),
         scratch_shapes=[
             pltpu.VMEM((6, EX, EY, F, NZ), jnp.float32),
             pltpu.VMEM((2, EX, EY, 1, NZ), jnp.float32),
             pltpu.VMEM((2, 4, NX, NY, 1, NZ), jnp.float32),
             pltpu.VMEM((2 * NZ, NZ), jnp.bfloat16),
+            pltpu.VMEM((F * rows, NZ), jnp.float32),
+            pltpu.VMEM((rows, NZ), jnp.float32),
             dma((4, 2, 4)),
             dma((4, 2, 4)),
             dma((4, 6, 2)),
             dma((4, 6, 2)),
             dma((4, 2, 3, 2)),
             dma((4, 2, 3, 2)),
-            dma((2, 3)),
-            dma((2, 3)),
+            dma((2, 6, 3)),
+            dma((2, 6, 3)),
+            dma((3, 3)),
+            dma((3,)),
+            dma((2,)),
         ],
         compiler_params=pltpu.CompilerParams(
             collective_id=0, has_side_effects=True, vmem_limit_bytes=40 * 1024 * 1024
         ),
         name="etrs",
-    )(orbitals.reshape(F * rows, NZ), external.reshape(rows, NZ))
-    return out.reshape(orbitals.shape), pot.reshape(external.shape)
+    )(
+        pltpu.with_memory_space_constraint(orbitals.transpose(0, 1, 3, 2, 4).reshape(F * rows, NZ), pltpu.HBM),
+        pltpu.with_memory_space_constraint(external.transpose(1, 0, 2).reshape(rows, NZ), pltpu.HBM),
+    )
+    out = out.reshape(2, F // 2, NY, NX, NZ).transpose(0, 1, 3, 2, 4)
+    return out, pot.reshape(NY, NX, NZ).transpose(1, 0, 2)
 
 
 def solution(mesh):

time: 116 us -> 101 us (0.87)
  the two profiles are of different devices: /device:TPU:58 before, /device:TPU:38 now
where the time goes in v3:
time: 101 us
  Pallas kernels  98.8 us (98%)
  local copies, waits for them, and re-layouts  1.37 us (1%)
    pallas_call x1, Pallas kernels, body(): pl.pallas_call(kernel, out_shape=(jax.ShapeDtypeStruct((F * rows, NZ), jn...  98.8 us

profile of v3, /device:TPU:38, one launch (start us, length us, event | category | flops | bytes accessed | tf_op | source)
XLA Modules:
  0.0 100.8 jit_solution(15387030426312821144)
XLA Ops:
  0.6 98.8 %etrs.1 = (f32[768,128]{1,0:T(8,128)S(1)}, f32[96,128]{1,0:T(8,128)S(1)}) custom-call(f32[768,128]{1,0:T(8,128)} %bitcast.14, f32[96,128]{1,0:T(8,128)} %bitcast.15), custom_call_target="tpu_custom_call" | custom-call | tf_op jit(solution)/shard_map/etrs/pallas_call | solution.py:492
  99.5 0.7 copy.6
  100.2 0.6 copy.7

commit v4 on v3

--- a/solution.py
+++ b/solution.py
@@ -16,7 +16,9 @@
 F = 8
 NX, NY, NZ = 8, 12, 128
 H = 8
-EX, EY = NX + 2 * H, NY + 2 * H
+M = 0
+HY = H + 2 * M
+EX, EY = NX + 2 * H, NY + 2 * HY
 
 
 def cube_root(x):
@@ -76,7 +78,7 @@
 
     def take_in(x, y):
         u = orb[pl.ds(y * NX + x, F, stride=NX * NY), :]
-        S[0, H + x, H + y] = u
+        S[0, H + x, HY + y] = u
         D[0, band, x, y] = density_of(u)
 
     off = jnp.abs(lax.broadcasted_iota(jnp.int32, (NZ, NZ), 0) - lax.broadcasted_iota(jnp.int32, (NZ, NZ), 1))
@@ -110,8 +112,8 @@
 
     pl.when(gx == 0)(lambda: clear_x(H - 2))
     pl.when(gx == n_gx - 1)(lambda: clear_x(H + NX))
-    pl.when(gy == 0)(lambda: clear_y(H - 2))
-    pl.when(gy == n_gy - 1)(lambda: clear_y(H + NY))
+    pl.when(gy == 0)(lambda: clear_y(HY - 2))
+    pl.when(gy == n_gy - 1)(lambda: clear_y(HY + NY))
 
     with jax.named_scope('barrier'):
         pl.semaphore_wait(bar, count)
@@ -122,7 +124,7 @@
         )
 
     def row_of(pair):
-        return jnp.where(odd == 1, H + NY - 2 - 2 * pair, H + 2 * pair)
+        return jnp.where(odd == 1, HY + NY - 2 - 2 * pair, HY + 2 * pair)
 
     def ref_of(e):
         return S.at[e] if e < 2 else V.at[e - 2]
@@ -130,10 +132,21 @@
     def reach(e):
         return 4 if e < 2 else 3
 
+    def pieces_of(e, side):
+        more = M if side == 1 and e in (0, 2) else 0
+        return range(M + 1 if side == 1 and e == 1 else 1, reach(e) + more + 1)
+
+    def depth_of(e, side, j):
+        more = M if side == 1 and e in (0, 2) else 0
+        return 2 * min(reach(e), reach(e) + more - j)
+
+    def relays_of(e, side):
+        return [j for j in range(1, 4 + M) if depth_of(e, side, j) > 0]
+
     def y_copy(e, side, j):
         buf = ref_of(e)
-        src_y = jnp.where(y_right[side], H + NY - 2 * j, H + 2 * (j - 1))
-        dst_y = jnp.where(y_right[side], H - 2 * j, H + NY + 2 * (j - 1))
+        src_y = jnp.where(y_right[side], HY + NY - 2 * j, HY + 2 * (j - 1))
+        dst_y = jnp.where(y_right[side], HY - 2 * j, HY + NY + 2 * (j - 1))
         return remote(
             buf.at[pl.ds(H, NX), pl.ds(src_y, 2)],
             buf.at[pl.ds(H, NX), pl.ds(dst_y, 2)],
@@ -158,14 +171,14 @@
 
     def relay(e, side, j, d):
         buf = ref_of(e)
-        depth = 2 * (reach(e) - j)
-        src_y = jnp.where(y_right[side], H + NY - 2 * j, H + 2 * (j - 1))
-        dst_y = jnp.where(y_right[side], H - 2 * j, H + NY + 2 * (j - 1))
+        depth = depth_of(e, side, j)
+        src_y = jnp.where(y_right[side], HY + NY - 2 * j, HY + 2 * (j - 1))
+        dst_y = jnp.where(y_right[side], HY - 2 * j, HY + NY + 2 * (j - 1))
         if side == 0:
             dst_x = H - depth if d == 0 else H + NX
             src_x, dev = dst_x, at(y=y_gy[0])
         else:
-            dst_y = src_y = jnp.where(y_right[1], H + NY + 2 * (j - 1), H - 2 * j)
+            dst_y = src_y = jnp.where(y_right[1], HY + NY + 2 * (j - 1), HY - 2 * j)
             src_x = H if d == 0 else H + NX - depth
             dst_x = H + NX if d == 0 else H - depth
             dev = at(x=x_gx[d])
@@ -196,7 +209,7 @@
         def _():
             for j in pieces:
                 y_copy(e, 1, j).wait_recv()
-                if j < reach(e):
+                if depth_of(e, 1, j) > 0:
                     for d in range(2):
                         pl.when(x_there[d])(lambda j=j, d=d: relay(e, 1, j, d).start())
 
@@ -207,17 +220,17 @@
     def take_far_potential(pieces):
         for j in pieces:
 
-            @pl.when(far_there & (band == j - 1))
+            @pl.when(far_there & (band == (j - 1) % 4))
             def _(j=j):
                 y_copy(2, 1, j).wait_recv()
                 for i in range(1, n_band):
                     spread(j, i).start()
 
-            @pl.when(far_there & (band != j - 1))
+            @pl.when(far_there & (band != (j - 1) % 4))
             def _(j=j):
                 spread(j, 1).wait_recv()
 
-            if j < 3:
+            if depth_of(2, 1, j) > 0:
                 for d in range(2):
                     when_side(1, x_there[d])(lambda j=j, d=d: relay(2, 1, j, d).start())
 
@@ -246,13 +259,12 @@
 
     def drain(e):
         for side in range(2):
-
-            for j in range(1, reach(e) + 1):
+            for j in pieces_of(e, side):
                 if side == 0 or e != 2:
                     when_side(side)(lambda j=j, side=side: y_copy(e, side, j).wait_send())
                 else:
 
-                    @pl.when(far_there & (band == j - 1))
+                    @pl.when(far_there & (band == (j - 1) % 4))
                     def _(j=j):
                         y_copy(e, 1, j).wait_send()
                         for i in range(1, n_band):
@@ -262,7 +274,7 @@
 
                 @when_side(side, x_there[d])
                 def _(side=side, d=d):
-                    for j in range(1, reach(e)):
+                    for j in relays_of(e, side):
                         relay(e, side, j, d).wait_send()
 
         for d in range(2):
@@ -273,7 +285,7 @@
                     x_copy(e, pair, d).wait_send()
 
     def band_rows(t, whose, pair):
-        return D.at[t, whose, pl.ds(0, NX), pl.ds(row_of(pair) - H, 2)]
+        return D.at[t, whose, pl.ds(0, NX), pl.ds(row_of(pair) - HY, 2)]
 
     def band_copy(t, pair, i):
         part = band_rows(t, band, pair)
@@ -318,23 +330,27 @@
                         for dy in range(2):
                             S[dst, edge + dx, y0 + dy] = zero
 
-    def stage(t, j):
-        if j == 0:
+    def stage(t, j, after=False):
+        if after:
+            for k in range(1, 5):
+                unit(t, k, k, NX + 4 * (4 - k))
+            return
+        if j < 1:
             for k in range(1, 5):
 
                 def one_pair(pair, carry, k=k):
                     unit(t, k, pair, NX + 4 * (4 - k))
                     return carry
 
-                lax.fori_loop(k, 10 - k, one_pair, 0)
+                lax.fori_loop(k - j, 10 - k, one_pair, 0)
             return
 
-        def some(ks):
+        def some(ks, j=j):
             for k in ks:
-                unit(t, k, k - j, NX + 4 * (4 - k - max(j - k, 0)))
+                unit(t, k, k - j, NX + 4 * (4 - k - max(j - k - (0 if t else M), 0)))
 
         if j > 1:
-            pl.when(far_there)(lambda: some(range(1, j)))
+            pl.when(far_there)(lambda: some(range(1, min(j, 5))))
         some(range(j, 5))
 
     sub = lax.broadcasted_iota(jnp.int32, (F, NZ), 0)
@@ -351,23 +367,33 @@
         def step(i, carry):
             for dx in range(4):
                 for dy in range(2):
-                    body(4 * i + dx, y0 - H + dy)
+                    body(4 * i + dx, y0 - HY + dy)
             return carry
 
         lax.fori_loop(0, NX // 4, step, 0)
 
     def terms(t, x, y):
-        return [S[t, H + x, H + y]] + [S[k, H + x, H + y] for k in range(2, 6)]
+        return [S[t, H + x, HY + y]] + [S[k, H + x, HY + y] for k in range(2, 6)]
 
     def half_way(x, y):
         w = terms(0, x, y)
         D[1, band, x, y] = density_of(combine(step_length, w))
-        S[1, H + x, H + y] = combine(step_length / 2, w)
+        S[1, H + x, HY + y] = combine(step_length / 2, w)
+
+    def half_way_only(x, y):
+        S[1, H + x, HY + y] = combine(step_length / 2, terms(0, x, y))
+
+    def half_halo_row(pair):
+        @pl.when(far_there)
+        def _():
+            each_of(pair, half_way_only)
+            for d in range(2):
+                pl.when(x_there[d])(lambda d=d: relay(1, 1, -pair, d).start())
 
     def half_row(pair):
         each_of(pair, half_way)
         send_band(1, pair)
-        if 0 < pair < 4:
+        if M <= pair < 4:
             send_y(1, 1, [pair + 1])
         if pair > 1:
             send_y(1, 0, [6 - pair])
@@ -388,13 +414,13 @@
             v = ext[pl.ds(y * NX + x, 1), :] - exchange_coef * cube_root(total)
             if t == 1:
                 pot[pl.ds(y * NX + x, 1), :] = v
-            V[t, H + x, H + y] = v + centre
+            V[t, H + x, HY + y] = v + centre
 
         each_of(pair, cell)
-        if pair < 3:
-            mine = far_there & (band == pair) if t == 0 else far_there
+        if pair + 1 in pieces_of(t + 2, 1):
+            mine = far_there & (band == pair % 4) if t == 0 else far_there
             pl.when(mine)(lambda: y_copy(t + 2, 1, pair + 1).start())
-        else:
+        if pair > 2:
             send_y(t + 2, 0, [6 - pair])
         send_x(t + 2, [pair])
 
@@ -409,7 +435,7 @@
     with scope('pot0'):
         for pair in rows:
             potential_row(0, pair)
-    send_y(0, 1, [3, 4])
+    send_y(0, 1, range(3, 5 + M))
     with scope('far01'):
         take_far(0, [1])
     with scope('x0'):
@@ -418,60 +444,74 @@
     with scope('near0'):
         await_near(0)
         await_near(2)
-        await_relay(0, 0, [1, 2, 3])
-        await_relay(2, 0, [1, 2])
+        await_relay(0, 0, relays_of(0, 0))
+        await_relay(2, 0, relays_of(2, 0))
+    with scope('far02'):
+        take_far(0, [2])
     with scope('stage00'):
         stage(0, 0)
     with scope('half00'):
         half_row(5)
         half_row(4)
-    for j in range(1, 5):
+    for j in range(1, 5 + M):
         with scope(f'far0{j}'):
-            if j < 4:
-                take_far(0, [j + 1])
+            if j in relays_of(0, 1):
+                if j > 1 and j + 1 in relays_of(0, 1):
+                    take_far(0, [j + 1])
+            else:
+                take_far(0, [j])
+            if j in pieces_of(2, 1):
                 take_far_potential([j])
         with scope(f'farrelay0{j}'):
-            if j < 4:
+            if j in relays_of(0, 1):
                 await_relay(0, 1, [j])
-                if j > 1:
-                    await_relay(2, 1, [j - 1])
+            if j - 1 in relays_of(2, 1):
+                await_relay(2, 1, [j - 1])
         with scope(f'stage0{j}'):
             stage(0, j)
-            half_row(4 - j)
+            if j < 5:
+                half_row(4 - j)
+            else:
+                half_halo_row(4 - j)
         with scope(f'pot1{j}'):
             if j == 1:
                 potential_row(1, 5)
                 potential_row(1, 4)
-            else:
+            elif j < 5:
                 potential_row(1, 5 - j)
-
-    with scope('pot15'):
-        potential_row(1, 0)
-    send_y(1, 1, [1])
+            if j == 4:
+                potential_row(1, 0)
+
     with scope('far1a'):
-        take_far(1, [4, 3, 2])
-    with scope('x1'):
-        await_x(1, rows)
-        await_x(3, rows)
+        take_far(1, range(4, max(M, 1), -1))
     with scope('near1'):
+        await_x(1, [5, 4, 3, 2])
+        await_x(3, [5, 4, 3, 2])
         await_near(1)
         await_near(3)
-        await_relay(1, 0, [1, 2, 3])
-        await_relay(3, 0, [1, 2])
-    with scope('stage10'):
-        stage(1, 0)
+        await_x(1, [1])
+        await_x(3, [1])
+        await_relay(1, 0, relays_of(1, 0))
+        await_relay(3, 0, relays_of(3, 0))
+    with scope('stage1m'):
+        stage(1, -1)
         out_row(5)
-        out_row(4)
+    with scope('x1'):
+        await_x(1, [0])
     with scope('farV1'):
         take_far(3, [3, 2, 1])
         take_far(1, [1])
+    with scope('stage10'):
+        stage(1, 0, after=True)
+        out_row(4)
     with scope('farrelay1'):
-        await_relay(1, 1, [1, 2, 3])
+        await_x(3, [0])
+        await_relay(1, 1, relays_of(1, 1))
     with scope('stage11'):
         stage(1, 1)
         out_row(3)
     with scope('farrelayV1'):
-        await_relay(3, 1, [1, 2])
+        await_relay(3, 1, relays_of(3, 1))
     with scope('stages1'):
         for j in range(2, 5):
             stage(1, j)
@@ -504,16 +544,16 @@
             pltpu.VMEM((2 * NZ, NZ), jnp.bfloat16),
             pltpu.VMEM((F * rows, NZ), jnp.float32),
             pltpu.VMEM((rows, NZ), jnp.float32),
-            dma((4, 2, 4)),
-            dma((4, 2, 4)),
+            dma((4, 2, 4 + M)),
+            dma((4, 2, 4 + M)),
             dma((4, 6, 2)),
             dma((4, 6, 2)),
-            dma((4, 2, 3, 2)),
-            dma((4, 2, 3, 2)),
+            dma((4, 2, 3 + M, 2)),
+            dma((4, 2, 3 + M, 2)),
             dma((2, 6, 3)),
             dma((2, 6, 3)),
-            dma((3, 3)),
-            dma((3,)),
+            dma((3 + M, 3)),
+            dma((3 + M,)),
             dma((2,)),
         ],
         compiler_params=pltpu.CompilerParams(

time: 101 us -> 100 us (0.990)
  the two profiles are of different devices: /device:TPU:38 before, /device:TPU:68 now
where the time goes in v4:
time: 100 us
  Pallas kernels  98.1 us (98%)
  local copies, waits for them, and re-layouts  1.37 us (1%)
    pallas_call x1, Pallas kernels, body(): pl.pallas_call(kernel, out_shape=(jax.ShapeDtypeStruct((F * rows, NZ), jn...  98.1 us

profile of v4, /device:TPU:68, one launch (start us, length us, event | category | flops | bytes accessed | tf_op | source)
XLA Modules:
  0.0 100.1 jit_solution(837978710389987257)
XLA Ops:
  0.6 98.1 %etrs.1 = (f32[768,128]{1,0:T(8,128)S(1)}, f32[96,128]{1,0:T(8,128)S(1)}) custom-call(f32[768,128]{1,0:T(8,128)} %bitcast.14, f32[96,128]{1,0:T(8,128)} %bitcast.15), custom_call_target="tpu_custom_call" | custom-call | tf_op jit(solution)/shard_map/etrs/pallas_call | solution.py:532
  98.7 0.7 copy.6
  99.5 0.6 copy.7

commit v5 on v4

--- a/solution.py
+++ b/solution.py
@@ -499,8 +499,8 @@
     with scope('x1'):
         await_x(1, [0])
     with scope('farV1'):
-        take_far(3, [3, 2, 1])
         take_far(1, [1])
+        take_far(3, [2, 1, 3])
     with scope('stage10'):
         stage(1, 0, after=True)
         out_row(4)

time: 100 us -> 99.1 us (level)
  the two profiles are of different devices: /device:TPU:68 before, /device:TPU:2 now
where the time goes in v5:
time: 99.1 us; the launch traced here: 99 us
  Pallas kernels  97 us (98%)
  local copies, waits for them, and re-layouts  1.37 us (1%)
    pallas_call x1, Pallas kernels, body(): pl.pallas_call(kernel, out_shape=(jax.ShapeDtypeStruct((F * rows, NZ), jn...  97 us

profile of v5, /device:TPU:2, one launch (start us, length us, event | category | flops | bytes accessed | tf_op | source)
XLA Modules:
  0.0 99.0 jit_solution(9397469367217532462)
XLA Ops:
  0.6 97.0 %etrs.1 = (f32[768,128]{1,0:T(8,128)S(1)}, f32[96,128]{1,0:T(8,128)S(1)}) custom-call(f32[768,128]{1,0:T(8,128)} %bitcast.14, f32[96,128]{1,0:T(8,128)} %bitcast.15), custom_call_target="tpu_custom_call" | custom-call | tf_op jit(solution)/shard_map/etrs/pallas_call | solution.py:532
  97.6 0.7 copy.6
  98.4 0.6 copy.7
